TPU v7x, 8 devices: a whole 2x2x1 slice. The times are simulated.
8 devices in a mesh: mat: 1 (over z), dp: 8 (over y, x, core).
Axes of the slice: x: 2, y: 2, z: 1, core: 2. Of those that a mesh axis runs over, the one named last changes fastest.
Arguments:
- a_mat: bfloat16 [3072, 32768], P('mat', 'dp')
Outputs:
- output: float32 [8, 5, 384, 384], P(('mat', 'dp'))
All inputs are finite; a program needn't handle non-finite values.
Results may differ from a plain program's by a relative error of at most 0.001.
Values are sent between devices in bfloat16 or wider.
A program may use at most 1 GiB of HBM per device.

v0:
```python
import jax
import jax.numpy as jnp
from jax import lax
from jax.sharding import PartitionSpec as P


def packed_partial(blocks):
    groups = blocks.shape[0]
    blk_rows = blocks.shape[1]
    half = groups // 2
    slots = half + 1
    doubled = jnp.concatenate([blocks, blocks], axis=0)
    dev_ids = lax.broadcasted_iota(jnp.int32, (groups, 1, 1), 0)

    def slot_step(slot, packed):
        partner = lax.dynamic_slice_in_dim(doubled, groups - slot, groups, axis=0)
        block_prod = jnp.einsum('gik,gjk->gij', blocks, partner, preferred_element_type=jnp.float32)
        flipped = jnp.where(dev_ids < slot, jnp.swapaxes(block_prod, 1, 2), block_prod)
        keep_mask = jnp.logical_or(slot < half, dev_ids < half)
        return lax.dynamic_update_index_in_dim(packed, jnp.where(keep_mask, flipped, 0.0), slot, axis=1)

    packed = jnp.zeros((groups, slots, blk_rows, blk_rows), jnp.float32)
    return lax.fori_loop(0, slots, slot_step, packed)


def solution(mesh):
    groups = mesh.shape['dp']

    def local_gram(a_local):
        n_rows, local_cols = a_local.shape
        blocks = a_local.reshape(groups, n_rows // groups, local_cols)
        return lax.psum_scatter(packed_partial(blocks), 'dp', scatter_dimension=0, tiled=True)

    return jax.shard_map(local_gram, mesh=mesh, in_specs=(P('mat', 'dp'),), out_specs=P(('mat', 'dp')), check_vma=False)
```

profile of v0, /device:TPU:0, one launch (start us, length us, event | category | flops | bytes accessed | tf_op | source)
XLA Modules:
  0.0 362.8 jit_solution(4170577161672875685)
XLA Ops:
  6.5 0.0 reduce-scatter.2.cloned.1.call-start
  6.5 33.8 %pad_maximum_fusion = bf16[16,384,4096]{2,1,0:T(8,128)(2,1)} fusion(bf16[8,384,4096]{2,1,0:T(8,128)(2,1)} %bitcast.24), kind=kLoop, calls=%fused_computation.9 | loop fusion | flops 25165824 | bytes 75497472 | tf_op jit(solution)/shard_map/concatenate | solution.py:12
  40.4 173.5 %while.17 = (s32[]{:T(128)}, f32[8,5,384,384]{3,2,1,0:T(8,128)}, bf16[16,384,4096]{2,1,0:T(8,128)(2,1)}, bf16[8,384,4096]{2,1,0:T(8,128)(2,1)}, s32[]{:T(128)}, ...) while((s32[]{:T(128)}, f32[8,5,384,384]{3,2,1,0:T(8,128)}, ...), condition=%wide.region_1.2_spmd.clone.clone, body=%wide.region_0.1_spmd.clone.clone.sunk | while | flops 9666035712 | bytes 78643904 | solution.py:23
  40.4 22.1 %fusion.12 = f32[8,384,384]{2,1,0:T(8,128)} fusion(bf16[8,384,4096]{2,1,0:T(8,128)(2,1)} %get-tuple-element.225, bf16[16,384,4096]{2,1,0:T(8,128)(2,1)} %get-tuple-element.224, s32[]{:T(128)S(6)} %select_n.60), kind=kOutput, calls=%fused_computation.1.clone.1 | convolution fusion | flops 9663676416 | bytes 55050244 | tf_op jit(solution)/shard_map/while/body/eval_jaxpr/gik,gjk->gij/dot_general | solution.py:17
  62.5 6.1 %copy.7 = f32[8,384,384]{1,2,0:T(8,128)} copy(f32[8,384,384]{2,1,0:T(8,128)} %fusion.12) | data formatting | bytes 9437184 | tf_op jit(solution)/shard_map/while/body/eval_jaxpr/gik,gjk->gij/dot_general | solution.py:17
  68.6 6.5 %bitcast_dynamic-update-slice_fusion.2 = f32[8,5,384,384]{3,2,1,0:T(8,128)} fusion(f32[8,5,384,384]{3,2,1,0:T(8,128)} %get-tuple-element.214, s32[]{:T(128)} %get-tuple-element.213, f32[8,384,384]{2,1,0:T(8,128)} %fusion.12, f32[8,384,384]{1,2,0:T(8,128)} %copy.7, pred[8]{0:T(512)(128)(4,1)S(1)} %get-tuple-element.202, ...), kind=kLoop, calls=%fused_computation.3.clone.1 | loop fusion | flops 2359296 | bytes 14156304 | tf_op jit(solution)/shard_map/while/body/eval_jaxpr/jit(dynamic_update_index_in_dim)/dynamic_update_slice | solution.py:20
  75.1 22.1 %fusion.12 = f32[8,384,384]{2,1,0:T(8,128)} fusion(bf16[8,384,4096]{2,1,0:T(8,128)(2,1)} %get-tuple-element.225, bf16[16,384,4096]{2,1,0:T(8,128)(2,1)} %get-tuple-element.224, s32[]{:T(128)S(6)} %select_n.60), kind=kOutput, calls=%fused_computation.1.clone.1 | convolution fusion | flops 9663676416 | bytes 55050244 | tf_op jit(solution)/shard_map/while/body/eval_jaxpr/gik,gjk->gij/dot_general | solution.py:17
  97.2 6.1 %copy.7 = f32[8,384,384]{1,2,0:T(8,128)} copy(f32[8,384,384]{2,1,0:T(8,128)} %fusion.12) | data formatting | bytes 9437184 | tf_op jit(solution)/shard_map/while/body/eval_jaxpr/gik,gjk->gij/dot_general | solution.py:17
  103.3 6.5 %bitcast_dynamic-update-slice_fusion.2 = f32[8,5,384,384]{3,2,1,0:T(8,128)} fusion(f32[8,5,384,384]{3,2,1,0:T(8,128)} %get-tuple-element.214, s32[]{:T(128)} %get-tuple-element.213, f32[8,384,384]{2,1,0:T(8,128)} %fusion.12, f32[8,384,384]{1,2,0:T(8,128)} %copy.7, pred[8]{0:T(512)(128)(4,1)S(1)} %get-tuple-element.202, ...), kind=kLoop, calls=%fused_computation.3.clone.1 | loop fusion | flops 2359296 | bytes 14156304 | tf_op jit(solution)/shard_map/while/body/eval_jaxpr/jit(dynamic_update_index_in_dim)/dynamic_update_slice | solution.py:20
  109.8 22.1 %fusion.12 = f32[8,384,384]{2,1,0:T(8,128)} fusion(bf16[8,384,4096]{2,1,0:T(8,128)(2,1)} %get-tuple-element.225, bf16[16,384,4096]{2,1,0:T(8,128)(2,1)} %get-tuple-element.224, s32[]{:T(128)S(6)} %select_n.60), kind=kOutput, calls=%fused_computation.1.clone.1 | convolution fusion | flops 9663676416 | bytes 55050244 | tf_op jit(solution)/shard_map/while/body/eval_jaxpr/gik,gjk->gij/dot_general | solution.py:17
  131.9 6.1 %copy.7 = f32[8,384,384]{1,2,0:T(8,128)} copy(f32[8,384,384]{2,1,0:T(8,128)} %fusion.12) | data formatting | bytes 9437184 | tf_op jit(solution)/shard_map/while/body/eval_jaxpr/gik,gjk->gij/dot_general | solution.py:17
  138.0 6.6 %bitcast_dynamic-update-slice_fusion.2 = f32[8,5,384,384]{3,2,1,0:T(8,128)} fusion(f32[8,5,384,384]{3,2,1,0:T(8,128)} %get-tuple-element.214, s32[]{:T(128)} %get-tuple-element.213, f32[8,384,384]{2,1,0:T(8,128)} %fusion.12, f32[8,384,384]{1,2,0:T(8,128)} %copy.7, pred[8]{0:T(512)(128)(4,1)S(1)} %get-tuple-element.202, ...), kind=kLoop, calls=%fused_computation.3.clone.1 | loop fusion | flops 2359296 | bytes 14156304 | tf_op jit(solution)/shard_map/while/body/eval_jaxpr/jit(dynamic_update_index_in_dim)/dynamic_update_slice | solution.py:20
  144.6 22.1 %fusion.12 = f32[8,384,384]{2,1,0:T(8,128)} fusion(bf16[8,384,4096]{2,1,0:T(8,128)(2,1)} %get-tuple-element.225, bf16[16,384,4096]{2,1,0:T(8,128)(2,1)} %get-tuple-element.224, s32[]{:T(128)S(6)} %select_n.60), kind=kOutput, calls=%fused_computation.1.clone.1 | convolution fusion | flops 9663676416 | bytes 55050244 | tf_op jit(solution)/shard_map/while/body/eval_jaxpr/gik,gjk->gij/dot_general | solution.py:17
  166.7 6.1 %copy.7 = f32[8,384,384]{1,2,0:T(8,128)} copy(f32[8,384,384]{2,1,0:T(8,128)} %fusion.12) | data formatting | bytes 9437184 | tf_op jit(solution)/shard_map/while/body/eval_jaxpr/gik,gjk->gij/dot_general | solution.py:17
  172.8 6.5 %bitcast_dynamic-update-slice_fusion.2 = f32[8,5,384,384]{3,2,1,0:T(8,128)} fusion(f32[8,5,384,384]{3,2,1,0:T(8,128)} %get-tuple-element.214, s32[]{:T(128)} %get-tuple-element.213, f32[8,384,384]{2,1,0:T(8,128)} %fusion.12, f32[8,384,384]{1,2,0:T(8,128)} %copy.7, pred[8]{0:T(512)(128)(4,1)S(1)} %get-tuple-element.202, ...), kind=kLoop, calls=%fused_computation.3.clone.1 | loop fusion | flops 2359296 | bytes 14156304 | tf_op jit(solution)/shard_map/while/body/eval_jaxpr/jit(dynamic_update_index_in_dim)/dynamic_update_slice | solution.py:20
  179.3 22.1 %fusion.12 = f32[8,384,384]{2,1,0:T(8,128)} fusion(bf16[8,384,4096]{2,1,0:T(8,128)(2,1)} %get-tuple-element.225, bf16[16,384,4096]{2,1,0:T(8,128)(2,1)} %get-tuple-element.224, s32[]{:T(128)S(6)} %select_n.60), kind=kOutput, calls=%fused_computation.1.clone.1 | convolution fusion | flops 9663676416 | bytes 55050244 | tf_op jit(solution)/shard_map/while/body/eval_jaxpr/gik,gjk->gij/dot_general | solution.py:17
  201.4 6.1 %copy.7 = f32[8,384,384]{1,2,0:T(8,128)} copy(f32[8,384,384]{2,1,0:T(8,128)} %fusion.12) | data formatting | bytes 9437184 | tf_op jit(solution)/shard_map/while/body/eval_jaxpr/gik,gjk->gij/dot_general | solution.py:17
  207.5 6.4 %bitcast_dynamic-update-slice_fusion.2 = f32[8,5,384,384]{3,2,1,0:T(8,128)} fusion(f32[8,5,384,384]{3,2,1,0:T(8,128)} %get-tuple-element.214, s32[]{:T(128)} %get-tuple-element.213, f32[8,384,384]{2,1,0:T(8,128)} %fusion.12, f32[8,384,384]{1,2,0:T(8,128)} %copy.7, pred[8]{0:T(512)(128)(4,1)S(1)} %get-tuple-element.202, ...), kind=kLoop, calls=%fused_computation.3.clone.1 | loop fusion | flops 2359296 | bytes 14156304 | tf_op jit(solution)/shard_map/while/body/eval_jaxpr/jit(dynamic_update_index_in_dim)/dynamic_update_slice | solution.py:20
  213.9 0.0 reduce-scatter.2.cloned.1.call-update
  213.9 142.0 %reduce-scatter.2.cloned.1.call-done = f32[1,5,384,384]{3,2,1,0:T(8,128)} async-done(((f32[8,5,384,384]{3,2,1,0:T(8,128)}), f32[1,5,384,384]{3,2,1,0:T(8,128)}) %reduce-scatter.2.cloned.1.call-update) | async-done | bytes 2949136 | tf_op jit(solution)/shard_map/reduce_scatter | solution.py:32
  (6 shorter events, 0.0 us)
Async XLA Ops:
  6.5 349.4 %reduce-scatter.2.cloned.1.call-start = ((), (), s32[]{:S(2)}) async-start(), calls=%async_computation.1 | async-start | bytes 26542080 | tf_op jit(solution)/shard_map/reduce_scatter | solution.py:32
Sparse Core Ops, SparseCore 0:
  214.1 141.8 reduce-scatter.1
where the time goes:
time: 363 us
  waiting for transfers between devices  142 us (39%)
  matrix products  110 us (30%)
  other arithmetic  66.3 us (18%)
  local copies, waits for them, and re-layouts  30.6 us (8%)
  between operations  13.4 us (4%)
    reduce_scatter x1, waiting for transfers between devices, local_gram(): lax.psum_scatter(packed_partial(blocks), 'dp', scatter_dimension=0, tiled...  142 us
    dot_general x5, matrix products, slot_step(): jnp.einsum('gik,gjk->gij', blocks, partner, preferred_element_type=jnp.fl...  110 us
    concatenate x1, other arithmetic, packed_partial(): doubled = jnp.concatenate([blocks, blocks], axis=0)  33.8 us
    dynamic_update_slice x5, other arithmetic, slot_step(): lax.dynamic_update_index_in_dim(packed, jnp.where(keep_mask, flipped, 0.0...  32.4 us
    dot_general x5, local copies, waits for them, and re-layouts, slot_step(): jnp.einsum('gik,gjk->gij', blocks, partner, preferred_element_type=jnp.fl...  30.6 us
  transfers between devices with their start and end apart: 1, of which 1 were waited for; matrix products, arithmetic and copies ran while one was open for 0% of the time, Pallas kernels for 0%

commit v1 on v0

v1 whole, which is shorter than its diff:
```python
import functools

import jax
import jax.numpy as jnp
from jax import lax
from jax.experimental import pallas as pl
from jax.experimental.pallas import tpu as pltpu
from jax.sharding import PartitionSpec as P

MESH = pl.DeviceIdType.MESH
BLK = 384
STRIP = 128
GROUPS = 8
SLOTS = 5
DIAG, ALONG_X, ALONG_Y, HERE = range(4)
STEPS = 20


def gram_kernel(a_hbm, out_ref, a_buf, acc, stage, from_x, from_y, relay_x, relay_y,
                load_sem, stage_sem, pair_sem, send_sem, fx_sem, fy_sem, rx_sem, ry_sem):
    me = lax.axis_index('dp')
    core = lax.rem(me, 2)
    x = lax.rem(me // 2, 2)
    y = me // 4

    def device(xx, yy, kk):
        return (yy * 2 + xx) * 2 + kk

    pair = device(x, y, 1 - core)
    nbr_x = device(1 - x, y, core)
    nbr_y = device(x, 1 - y, core)

    barrier = pltpu.get_barrier_semaphore()
    for other in (pair, nbr_x, nbr_y):
        pl.semaphore_signal(barrier, inc=1, device_id={'dp': other}, device_id_type=MESH)

    far = device(1 - x, 1 - y, 0)

    def load(n):
        if isinstance(n, int) and n < 2:
            row = far + (1 - core if n == 0 else core)
        else:
            row = lax.rem(far + 1 - n + GROUPS, GROUPS)
        rows = pl.ds(pl.multiple_of(row * BLK, BLK), BLK)
        return pltpu.make_async_copy(a_hbm.at[rows, :], a_buf.at[rows, :], load_sem.at[n])

    for n in range(GROUPS):
        load(n).start()

    def step_task(step):
        mid = step - SLOTS
        in_mid = jnp.logical_and(mid >= 0, mid < 2 * SLOTS)
        rel = jnp.where(step < SLOTS, DIAG, jnp.where(in_mid, ALONG_X + lax.rem(mid + 2 * SLOTS, 2), HERE))
        slot = jnp.where(step < SLOTS, step, jnp.where(in_mid, mid // 2, step - 3 * SLOTS))
        return rel, slot

    def dest_xy(rel):
        flip_x = jnp.where(rel <= ALONG_X, 1, 0)
        flip_y = jnp.where(lax.rem(rel, 2) == 0, 1, 0)
        xx = x + flip_x - 2 * flip_x * x
        yy = y + flip_y - 2 * flip_y * y
        return xx, yy

    def exists(rel, slot):
        _, yy = dest_xy(rel)
        return jnp.logical_or(slot < SLOTS - 1, yy == 0)

    def product(rel, slot, kk):
        xx, yy = dest_xy(rel)
        p = device(xx, yy, kk)
        q = lax.rem(p - slot + GROUPS, GROUPS)
        hi = pl.multiple_of(jnp.maximum(p, q) * BLK, BLK)
        lo = pl.multiple_of(jnp.minimum(p, q) * BLK, BLK)
        return lax.dot_general(a_buf[pl.ds(hi, BLK), :], a_buf[pl.ds(lo, BLK), :],
                               (((1,), (1,)), ((), ())), preferred_element_type=jnp.float32)

    def pair_copy(step):
        rel, slot = step_task(step)
        return pltpu.make_async_remote_copy(
            src_ref=stage.at[lax.rem(step, 2)], dst_ref=acc.at[rel, slot],
            send_sem=stage_sem.at[lax.rem(step, 2)], recv_sem=pair_sem.at[rel, slot],
            device_id={'dp': pair}, device_id_type=MESH)

    def pair_step(step):
        rel, slot = step_task(step)

        @pl.when(exists(rel, slot))
        def _():
            stage[lax.rem(step, 2)] = product(rel, slot, 1 - core)
            pair_copy(step).start()

    def by_y(ordinal, dest_y):
        long_n, long_o = 5 + core, 4 - 2 * core
        short = ((ordinal + 1) * 7) // 11 - (ordinal * 7) // 11
        full = ((ordinal + 1) * long_n + long_o) // 14 - (ordinal * long_n + long_o) // 14
        return jnp.where(dest_y == 1, short, full) == 1

    def strip(m):
        return pl.ds(m * STRIP, STRIP)

    def ordinal(slot, m):
        return jnp.where(slot == 0, m // 2, 3 * slot - 1 + m)

    def sent(slot, m):
        return slot >= (1 if m == 1 else 0)

    def far_send(slot, m, along_y):
        return pltpu.make_async_remote_copy(
            src_ref=acc.at[DIAG, slot, strip(m)],
            dst_ref=(relay_x if along_y else relay_y).at[slot, strip(m)],
            send_sem=send_sem.at[DIAG, slot, m],
            recv_sem=(rx_sem if along_y else ry_sem).at[slot, m],
            device_id={'dp': nbr_y if along_y else nbr_x}, device_id_type=MESH)

    def near_send(rel, slot, m):
        along_y = rel == ALONG_Y
        return pltpu.make_async_remote_copy(
            src_ref=acc.at[rel, slot, strip(m)],
            dst_ref=(from_y if along_y else from_x).at[slot, strip(m)],
            send_sem=send_sem.at[rel, slot, m],
            recv_sem=(fy_sem if along_y else fx_sem).at[slot, m],
            device_id={'dp': nbr_y if along_y else nbr_x}, device_id_type=MESH)

    def own_step(step):
        rel, slot = step_task(step)

        @pl.when(exists(rel, slot))
        def _():
            pair_copy(step).wait_recv()
            acc[rel, slot] = acc[rel, slot] + product(rel, slot, core)

            @pl.when(slot == 0)
            def _():
                acc[rel, slot, 0:STRIP, STRIP:] = acc[rel, slot, STRIP:2 * STRIP, :2 * STRIP]

            for m in range(3):
                @pl.when(jnp.logical_and(rel == DIAG, sent(slot, m)))
                def _(m=m):
                    along_y = by_y(ordinal(slot, m), 1 - y)

                    @pl.when(along_y)
                    def _():
                        far_send(slot, m, True).start()

                    @pl.when(jnp.logical_not(along_y))
                    def _():
                        far_send(slot, m, False).start()

                @pl.when(jnp.logical_and(rel == ALONG_X, sent(slot, m)))
                def _(m=m):
                    @pl.when(by_y(ordinal(slot, m), y))
                    def _():
                        far_send(slot, m, True).wait_recv()
                        acc[ALONG_X, slot, strip(m)] = acc[ALONG_X, slot, strip(m)] + relay_x[slot, strip(m)]

                    near_send(ALONG_X, slot, m).start()

                @pl.when(jnp.logical_and(rel == ALONG_Y, sent(slot, m)))
                def _(m=m):
                    @pl.when(jnp.logical_not(by_y(ordinal(slot, m), 1 - y)))
                    def _():
                        far_send(slot, m, False).wait_recv()
                        acc[ALONG_Y, slot, strip(m)] = acc[ALONG_Y, slot, strip(m)] + relay_y[slot, strip(m)]

                    near_send(ALONG_Y, slot, m).start()

    load(0).wait()
    first = product(DIAG, 0, 1 - core)
    stage[0] = first
    pl.semaphore_wait(barrier, 3)
    pair_copy(0).start()
    load(1).wait()
    own_step(0)
    load(2).wait()
    pair_step(1)

    def body(step, carry):
        @pl.when(step < SLOTS)
        def _():
            load(step + 2).wait()

        @pl.when(step == SLOTS - 1)
        def _():
            load(GROUPS - 1).wait()

        @pl.when(step < STEPS - 1)
        def _():
            @pl.when(exists(*step_task(step - 1)))
            def _():
                pair_copy(step - 1).wait_send()

            pair_step(step + 1)

        own_step(step)
        return carry

    lax.fori_loop(1, STEPS, body, 0)

    for step in (STEPS - 2, STEPS - 1):
        @pl.when(exists(*step_task(step)))
        def _(step=step):
            pair_copy(step).wait_send()

    for slot in range(SLOTS):
        @pl.when(exists(HERE, slot))
        def _(slot=slot):
            for m in range(3):
                if slot == 0 and m == 1:
                    continue
                near_send(ALONG_X, slot, m).wait_recv()
                near_send(ALONG_Y, slot, m).wait_recv()
                total = acc[HERE, slot, strip(m)] + from_x[slot, strip(m)] + from_y[slot, strip(m)]
                if slot:
                    out_ref[0, slot, strip(m)] = total
                elif m == 0:
                    out_ref[0, 0, 0:STRIP, 0:STRIP] = total[:, 0:STRIP]
                    out_ref[0, 0, STRIP:2 * STRIP, 0:2 * STRIP] = total[:, STRIP:]
                    out_ref[0, 0, 0:STRIP, STRIP:2 * STRIP] = total[:, STRIP:2 * STRIP].T
                else:
                    out_ref[0, 0, strip(2)] = total
                    out_ref[0, 0, 0:STRIP, 2 * STRIP:] = total[:, 0:STRIP].T
                    out_ref[0, 0, STRIP:2 * STRIP, 2 * STRIP:] = total[:, STRIP:2 * STRIP].T

        if slot == SLOTS - 1:
            @pl.when(jnp.logical_not(exists(HERE, slot)))
            def _(slot=slot):
                out_ref[0, slot] = jnp.zeros((BLK, BLK), jnp.float32)

    for rel in (DIAG, ALONG_X, ALONG_Y):
        for slot in range(SLOTS):
            @pl.when(exists(rel, slot))
            def _(rel=rel, slot=slot):
                for m in range(3):
                    if slot == 0 and m == 1:
                        continue
                    if rel == DIAG:
                        far_send(slot, m, True).wait_send()
                    else:
                        near_send(rel, slot, m).wait_send()


def solution(mesh):
    def local_gram(a_local):
        block = (SLOTS, BLK, BLK)
        dma = pltpu.SemaphoreType.DMA
        return pl.pallas_call(
            gram_kernel,
            out_shape=jax.ShapeDtypeStruct((1,) + block, jnp.float32),
            in_specs=[pl.BlockSpec(memory_space=pl.ANY)],
            out_specs=pl.BlockSpec(memory_space=pltpu.VMEM),
            scratch_shapes=[
                pltpu.VMEM(a_local.shape, a_local.dtype),
                pltpu.VMEM((4,) + block, jnp.float32),
                pltpu.VMEM((2, BLK, BLK), jnp.float32),
                pltpu.VMEM(block, jnp.float32),
                pltpu.VMEM(block, jnp.float32),
                pltpu.VMEM(block, jnp.float32),
                pltpu.VMEM(block, jnp.float32),
                dma((GROUPS,)),
                dma((2,)),
                dma((4, SLOTS)),
                dma((3, SLOTS, 3)),
                dma((SLOTS, 3)),
                dma((SLOTS, 3)),
                dma((SLOTS, 3)),
                dma((SLOTS, 3)),
            ],
            compiler_params=pltpu.CompilerParams(
                collective_id=0, has_side_effects=True, vmem_limit_bytes=67043328),
        )(a_local)

    return jax.shard_map(local_gram, mesh=mesh, in_specs=(P('mat', 'dp'),), out_specs=P(('mat', 'dp')), check_vma=False)
```

time: 363 us -> 102 us (0.28)
  waiting for transfers between devices: 142 us -> 0 us
  matrix products: 110 us -> 0 us
  Pallas kernels: 0 us -> 98.5 us
  other arithmetic: 66.3 us -> 0 us
  local copies, waits for them, and re-layouts: 30.6 us -> 3.63 us
  between operations: 13.4 us -> 0.01 us
    reduce_scatter x1 -> x0, waiting for transfers between devices: 142 us -> none  [local_gram(): lax.psum_scatter(packed_partial(blocks), 'dp', scatter_dimension=0, tiled...]
    dot_general x5 -> x0, matrix products: 110 us -> none  [slot_step(): jnp.einsum('gik,gjk->gij', blocks, partner, preferred_element_type=jnp.fl...]
    pallas_call x0 -> x1, Pallas kernels: none -> 98.5 us  [local_gram(): pl.pallas_call(gram_kernel, out_shape=jax.ShapeDtypeStruct((1,) + block,...]
    concatenate x1 -> x0, other arithmetic: 33.8 us -> none  [packed_partial(): doubled = jnp.concatenate([blocks, blocks], axis=0)]
    dynamic_update_slice x5 -> x0, other arithmetic: 32.4 us -> none  [slot_step(): lax.dynamic_update_index_in_dim(packed, jnp.where(keep_mask, flipped, 0.0...]
    dot_general x5 -> x0, local copies, waits for them, and re-layouts: 30.6 us -> none  [slot_step(): jnp.einsum('gik,gjk->gij', blocks, partner, preferred_element_type=jnp.fl...]
  transfers between devices with their start and end apart: 1 -> 0, of which waited for: 1 -> 0; matrix products, arithmetic and copies ran while one was open for 0% -> 0% of each run, Pallas kernels for 0% -> 0%
where the time goes in v1:
time: 102 us
  Pallas kernels  98.5 us (97%)
  local copies, waits for them, and re-layouts  3.63 us (4%)
    pallas_call x1, Pallas kernels, local_gram(): pl.pallas_call(gram_kernel, out_shape=jax.ShapeDtypeStruct((1,) + block,...  98.5 us
    unnamed x1, local copies, waits for them, and re-layouts  3.63 us

profile of v1, /device:TPU:0, one launch (start us, length us, event | category | flops | bytes accessed | tf_op | source)
XLA Modules:
  0.0 102.1 jit_solution(1450862636003233195)
XLA Ops:
  0.0 98.5 %shard_map.17 = f32[1,5,384,384]{3,2,1,0:T(8,128)} custom-call(bf16[3072,4096]{1,0:T(8,128)(2,1)} %a_hbm.1), custom_call_target="tpu_custom_call" | custom-call | tf_op jit(solution)/shard_map/pallas_call | solution.py:246
  98.5 3.6 %copy.3 = f32[1,5,384,384]{3,2,1,0:T(8,128)} copy(f32[1,5,384,384]{3,2,1,0:T(8,128)} %shard_map.17) | data formatting | bytes 5898240

commit v2 on v0

v2 whole, which is shorter than its diff:
```python
import functools

import jax
import jax.numpy as jnp
from jax import lax
from jax.experimental import pallas as pl
from jax.experimental.pallas import tpu as pltpu
from jax.sharding import PartitionSpec as P

MESH = pl.DeviceIdType.MESH
BLK = 384
STRIP = 128
GROUPS = 8
SLOTS = 5
DIAG, ALONG_X, ALONG_Y, HERE = range(4)
STEPS = 20


def pack_symmetric(ref):
    row = lax.broadcasted_iota(jnp.int32, (STRIP, STRIP), 0)
    col = lax.broadcasted_iota(jnp.int32, (STRIP, STRIP), 1)
    s11 = ref[STRIP:2 * STRIP, STRIP:2 * STRIP]
    main = jnp.sum(jnp.where(row == col, s11, 0.0), axis=0, keepdims=True)
    ref[0:STRIP, 0:STRIP] = jnp.where(row >= col, ref[0:STRIP, 0:STRIP], s11)
    ref[0:STRIP, STRIP:2 * STRIP] = ref[STRIP:2 * STRIP, 0:STRIP]
    ref[0:STRIP, 2 * STRIP:] = ref[2 * STRIP:, 0:STRIP]
    ref[STRIP:2 * STRIP, 0:STRIP] = ref[2 * STRIP:, STRIP:2 * STRIP]
    ref[STRIP:2 * STRIP, STRIP:2 * STRIP] = jnp.where(
        row >= col, ref[2 * STRIP:, 2 * STRIP:], jnp.where(row == 0, main, s11[0:1, 0:1]))


def unpack_symmetric(ref, top, low):
    row = lax.broadcasted_iota(jnp.int32, (STRIP, STRIP), 0)
    col = lax.broadcasted_iota(jnp.int32, (STRIP, STRIP), 1)
    both, s10, s20 = top[:, 0:STRIP], top[:, STRIP:2 * STRIP], top[:, 2 * STRIP:]
    s21, last = low[:, 0:STRIP], low[:, STRIP:]
    both_t, last_t = both.T, last.T
    main = jnp.where(col[0:1] == 0, last[1:2, STRIP - 1:STRIP], last[0:1, :])
    ref[0:STRIP, 0:STRIP] = jnp.where(row >= col, both, both_t)
    ref[STRIP:2 * STRIP, STRIP:2 * STRIP] = jnp.where(row == col, main, jnp.where(row < col, both, both_t))
    ref[2 * STRIP:, 2 * STRIP:] = jnp.where(row >= col, last, last_t)
    ref[STRIP:2 * STRIP, 0:STRIP] = s10
    ref[0:STRIP, STRIP:2 * STRIP] = s10.T
    ref[2 * STRIP:, 0:STRIP] = s20
    ref[0:STRIP, 2 * STRIP:] = s20.T
    ref[2 * STRIP:, STRIP:2 * STRIP] = s21
    ref[STRIP:2 * STRIP, 2 * STRIP:] = s21.T


def gram_kernel(a_hbm, out_ref, a_buf, acc, stage, mine, from_x, from_y, relay_x, relay_y,
                load_sem, stage_sem, pair_sem, send_sem, fx_sem, fy_sem, rx_sem, ry_sem):
    me = lax.axis_index('dp')
    core = lax.rem(me, 2)
    x = lax.rem(me // 2, 2)
    y = me // 4
    half = a_buf.shape[1] // 2

    def device(xx, yy, kk):
        return (yy * 2 + xx) * 2 + kk

    pair = device(x, y, 1 - core)
    nbr_x = device(1 - x, y, core)
    nbr_y = device(x, 1 - y, core)

    barrier = pltpu.get_barrier_semaphore()
    for other in (pair, nbr_x, nbr_y):
        pl.semaphore_signal(barrier, inc=1, device_id={'dp': other}, device_id_type=MESH)

    far = device(1 - x, 1 - y, 0)

    def load(n, part=None):
        if isinstance(n, int) and n < 2:
            row = far + (1 - core if n == 0 else core)
        else:
            row = lax.rem(far + 1 - n + GROUPS, GROUPS)
        rows = pl.ds(pl.multiple_of(row * BLK, BLK), BLK)
        if part is None:
            return pltpu.make_async_copy(a_hbm.at[rows, :], a_buf.at[rows, :], load_sem.at[n])
        cols = pl.ds(part * half, half)
        return pltpu.make_async_copy(a_hbm.at[rows, cols], a_buf.at[rows, cols], load_sem.at[GROUPS * part])

    load(0, 0).start()
    load(0, 1).start()
    for n in range(1, GROUPS):
        load(n).start()

    near_first = ALONG_X + y
    near_second = ALONG_Y - y

    def step_task(step):
        mid = step - SLOTS
        in_mid = jnp.logical_and(mid >= 0, mid < 2 * SLOTS)
        near = jnp.where(lax.rem(mid + 2 * SLOTS, 2) == 0, near_first, near_second)
        rel = jnp.where(step < SLOTS, DIAG, jnp.where(in_mid, near, HERE))
        slot = jnp.where(step < SLOTS, step, jnp.where(in_mid, mid // 2, step - 3 * SLOTS))
        return rel, slot

    def dest_xy(rel):
        flip_x = jnp.where(rel <= ALONG_X, 1, 0)
        flip_y = jnp.where(lax.rem(rel, 2) == 0, 1, 0)
        xx = x + flip_x - 2 * flip_x * x
        yy = y + flip_y - 2 * flip_y * y
        return xx, yy

    def exists(rel, slot):
        _, yy = dest_xy(rel)
        return jnp.logical_or(slot < SLOTS - 1, yy == 0)

    def dot(lo, lo_rows, hi, hi_rows, cols=slice(None)):
        return lax.dot_general(a_buf[pl.ds(lo, lo_rows), cols], a_buf[pl.ds(hi, hi_rows), cols],
                               (((1,), (1,)), ((), ())), preferred_element_type=jnp.float32)

    def product(rel, slot, kk):
        xx, yy = dest_xy(rel)
        p = device(xx, yy, kk)
        q = lax.rem(p - slot + GROUPS, GROUPS)
        hi = pl.multiple_of(jnp.maximum(p, q) * BLK, BLK)
        lo = pl.multiple_of(jnp.minimum(p, q) * BLK, BLK)
        return dot(hi, BLK, lo, BLK)

    def pair_copy(step, rows=BLK):
        rel, slot = step_task(step)
        rows = pl.ds(0, rows)
        return pltpu.make_async_remote_copy(
            src_ref=stage.at[lax.rem(step, 2), rows], dst_ref=acc.at[rel, slot, rows],
            send_sem=stage_sem.at[lax.rem(step, 2)], recv_sem=pair_sem.at[rel, slot],
            device_id={'dp': pair}, device_id_type=MESH)

    def by_y(ordinal, dest_y):
        later = ordinal - 2
        long_n, long_o = 4 + core, 8 - core
        short = (later * 2 + 3) // 3 - (later * 2 + 1) // 3
        full = ((later + 1) * long_n + long_o) // 12 - (later * long_n + long_o) // 12
        rest = jnp.where(dest_y == 1, short, full)
        return jnp.where(ordinal < 2, lax.rem(ordinal + core, 2), rest) == 1

    def piece(ref, m, first):
        rows = pl.ds(m * STRIP, STRIP)
        if first and m == 1:
            return ref.at[rows, pl.ds(0, 2 * STRIP)]
        return ref.at[rows, :]

    def pieces(first):
        return range(2 if first else 3)

    def ordinal(slot, m, first):
        return m if first else 3 * slot - 1 + m

    def far_send(slot, m, first, along_y):
        return pltpu.make_async_remote_copy(
            src_ref=piece(acc.at[DIAG, slot], m, first),
            dst_ref=piece((relay_x if along_y else relay_y).at[slot], m, first),
            send_sem=send_sem.at[DIAG, slot, m],
            recv_sem=(rx_sem if along_y else ry_sem).at[slot, m],
            device_id={'dp': nbr_y if along_y else nbr_x}, device_id_type=MESH)

    def near_send(rel, slot, m, first):
        along_y = rel == ALONG_Y
        return pltpu.make_async_remote_copy(
            src_ref=piece(acc.at[rel, slot], m, first),
            dst_ref=piece((from_y if along_y else from_x).at[slot], m, first),
            send_sem=send_sem.at[rel, slot, m],
            recv_sem=(fy_sem if along_y else fx_sem).at[slot, m],
            device_id={'dp': nbr_y if along_y else nbr_x}, device_id_type=MESH)

    def finish(rel, slot, first, only_far=False):
        for m in pieces(first):
            block = piece(acc.at[rel, slot], m, first)
            block[...] = block[...] + piece(mine, m, first)[...]

            def send_far(m=m):
                along_y = by_y(ordinal(slot, m, first), 1 - y)

                @pl.when(along_y)
                def _():
                    far_send(slot, m, first, True).start()

                @pl.when(jnp.logical_not(along_y))
                def _():
                    far_send(slot, m, first, False).start()

            if only_far:
                send_far()
                continue
            pl.when(rel == DIAG)(send_far)

            @pl.when(rel == ALONG_X)
            def _(m=m):
                @pl.when(by_y(ordinal(slot, m, first), y))
                def _():
                    far_send(slot, m, first, True).wait_recv()
                    total = piece(acc.at[ALONG_X, slot], m, first)
                    total[...] = total[...] + piece(relay_x.at[slot], m, first)[...]

                near_send(ALONG_X, slot, m, first).start()

            @pl.when(rel == ALONG_Y)
            def _(m=m):
                @pl.when(jnp.logical_not(by_y(ordinal(slot, m, first), 1 - y)))
                def _():
                    far_send(slot, m, first, False).wait_recv()
                    total = piece(acc.at[ALONG_Y, slot], m, first)
                    total[...] = total[...] + piece(relay_y.at[slot], m, first)[...]

                near_send(ALONG_Y, slot, m, first).start()

    def first_product(ref, kk, halves):
        row = pl.multiple_of((far + kk) * BLK, BLK)
        for h in range(halves):
            cols = pl.ds(h * half, half) if halves > 1 else slice(None)
            if halves > 1:
                load(0, h).wait()
            left = dot(row, BLK, row, 2 * STRIP, cols)
            corner = dot(row + 2 * STRIP, STRIP, row + 2 * STRIP, STRIP, cols)
            if h:
                left = ref[:, 0:2 * STRIP] + left
                corner = ref[2 * STRIP:, 2 * STRIP:] + corner
            ref[:, 0:2 * STRIP] = left
            ref[2 * STRIP:, 2 * STRIP:] = corner
        pack_symmetric(ref)

    first_product(stage.at[0], 1 - core, 2)
    pl.semaphore_wait(barrier, 3)
    pair_copy(0, 2 * STRIP).start()
    load(1).wait()
    first_product(mine, core, 1)
    pair_copy(0, 2 * STRIP).wait_recv()
    finish(DIAG, 0, True, only_far=True)

    def body(step, carry):
        @pl.when(step < SLOTS + 1)
        def _():
            load(step + 1).wait()

        @pl.when(step == SLOTS)
        def _():
            load(GROUPS - 1).wait()

        rel, slot = step_task(step)

        @pl.when(exists(rel, slot))
        def _():
            stage_now = stage.at[lax.rem(step, 2)]
            stage_now[...] = product(rel, slot, 1 - core)

            @pl.when(slot == 0)
            def _():
                pack_symmetric(stage_now)

            pair_copy(step).start()
            mine[...] = product(rel, slot, core)

            @pl.when(slot == 0)
            def _():
                pack_symmetric(mine)
                pair_copy(step).wait_recv()
                finish(rel, slot, True)

            @pl.when(slot > 0)
            def _():
                pair_copy(step).wait_recv()
                finish(rel, slot, False)

            pair_copy(step).wait_send()

        return carry

    pair_copy(0, 2 * STRIP).wait_send()
    lax.fori_loop(1, STEPS, body, 0)

    def arrived(slot, m, first):
        near_send(ALONG_X, slot, m, first).wait_recv()
        near_send(ALONG_Y, slot, m, first).wait_recv()
        return (piece(acc.at[HERE, slot], m, first)[...] + piece(from_x.at[slot], m, first)[...]
                + piece(from_y.at[slot], m, first)[...])

    unpack_symmetric(out_ref.at[0, 0], arrived(0, 0, True), arrived(0, 1, True))
    for slot in range(1, SLOTS):
        @pl.when(exists(HERE, slot))
        def _(slot=slot):
            for m in pieces(False):
                out_ref[0, slot, m * STRIP:(m + 1) * STRIP] = arrived(slot, m, False)

    @pl.when(jnp.logical_not(exists(HERE, SLOTS - 1)))
    def _():
        out_ref[0, SLOTS - 1] = jnp.zeros((BLK, BLK), jnp.float32)

    for rel in (DIAG, ALONG_X, ALONG_Y):
        for slot in range(SLOTS):
            @pl.when(exists(rel, slot))
            def _(rel=rel, slot=slot):
                first = slot == 0
                for m in pieces(first):
                    if rel == DIAG:
                        far_send(slot, m, first, True).wait_send()
                    else:
                        near_send(rel, slot, m, first).wait_send()


def solution(mesh):
    def local_gram(a_local):
        block = (SLOTS, BLK, BLK)
        dma = pltpu.SemaphoreType.DMA
        return pl.pallas_call(
            gram_kernel,
            out_shape=pltpu.VMEM((1,) + block, jnp.float32),
            in_specs=[pl.BlockSpec(memory_space=pl.ANY)],
            out_specs=pl.BlockSpec(memory_space=pltpu.VMEM),
            scratch_shapes=[
                pltpu.VMEM(a_local.shape, a_local.dtype),
                pltpu.VMEM((4,) + block, jnp.float32),
                pltpu.VMEM((2, BLK, BLK), jnp.float32),
                pltpu.VMEM((BLK, BLK), jnp.float32),
                pltpu.VMEM(block, jnp.float32),
                pltpu.VMEM(block, jnp.float32),
                pltpu.VMEM(block, jnp.float32),
                pltpu.VMEM(block, jnp.float32),
                dma((GROUPS + 1,)),
                dma((2,)),
                dma((4, SLOTS)),
                dma((3, SLOTS, 3)),
                dma((SLOTS, 3)),
                dma((SLOTS, 3)),
                dma((SLOTS, 3)),
                dma((SLOTS, 3)),
            ],
            compiler_params=pltpu.CompilerParams(
                collective_id=0, has_side_effects=True, vmem_limit_bytes=56623104),
        )(a_local)

    return jax.shard_map(local_gram, mesh=mesh, in_specs=(P('mat', 'dp'),), out_specs=P(('mat', 'dp')), check_vma=False)
```

time: 363 us -> 91.7 us (0.25)
  waiting for transfers between devices: 142 us -> 0 us
  matrix products: 110 us -> 0 us
  Pallas kernels: 0 us -> 89.3 us
  other arithmetic: 66.3 us -> 0 us
  local copies, waits for them, and re-layouts: 30.6 us -> 1.6 us
  between operations: 13.4 us -> 0.01 us
    reduce_scatter x1 -> x0, waiting for transfers between devices: 142 us -> none  [local_gram(): lax.psum_scatter(packed_partial(blocks), 'dp', scatter_dimension=0, tiled...]
    dot_general x5 -> x0, matrix products: 110 us -> none  [slot_step(): jnp.einsum('gik,gjk->gij', blocks, partner, preferred_element_type=jnp.fl...]
    pallas_call x0 -> x1, Pallas kernels: none -> 89.3 us  [local_gram(): pl.pallas_call(gram_kernel, out_shape=pltpu.VMEM((1,) + block, jnp.float3...]
    concatenate x1 -> x0, other arithmetic: 33.8 us -> none  [packed_partial(): doubled = jnp.concatenate([blocks, blocks], axis=0)]
    dynamic_update_slice x5 -> x0, other arithmetic: 32.4 us -> none  [slot_step(): lax.dynamic_update_index_in_dim(packed, jnp.where(keep_mask, flipped, 0.0...]
    dot_general x5 -> x0, local copies, waits for them, and re-layouts: 30.6 us -> none  [slot_step(): jnp.einsum('gik,gjk->gij', blocks, partner, preferred_element_type=jnp.fl...]
  transfers between devices with their start and end apart: 1 -> 0, of which waited for: 1 -> 0; matrix products, arithmetic and copies ran while one was open for 0% -> 0% of each run, Pallas kernels for 0% -> 0%
where the time goes in v2:
time: 91.7 us; the launch traced here: 90.9 us
  Pallas kernels  89.3 us (97%)
  local copies, waits for them, and re-layouts  1.6 us (2%)
    pallas_call x1, Pallas kernels, local_gram(): pl.pallas_call(gram_kernel, out_shape=pltpu.VMEM((1,) + block, jnp.float3...  89.3 us

profile of v2, /device:TPU:0, one launch (start us, length us, event | category | flops | bytes accessed | tf_op | source)
XLA Modules:
  0.0 90.9 jit_solution(10265171249340749327)
XLA Ops:
  0.0 89.3 %shard_map.17 = f32[1,5,384,384]{3,2,1,0:T(8,128)S(1)} custom-call(bf16[3072,4096]{1,0:T(8,128)(2,1)} %a_hbm.1), custom_call_target="tpu_custom_call" | custom-call | tf_op jit(solution)/shard_map/pallas_call | solution.py:304
  89.3 1.6 %copy.3 = f32[1,5,384,384]{3,2,1,0:T(8,128)} copy(f32[1,5,384,384]{3,2,1,0:T(8,128)S(1)} %shard_map.17) | data formatting | bytes 5898240

commit v3 on v2

v3 whole, which is shorter than its diff:
```python
import functools

import jax
import jax.numpy as jnp
from jax import lax
from jax.experimental import pallas as pl
from jax.experimental.pallas import tpu as pltpu
from jax.sharding import PartitionSpec as P

MESH = pl.DeviceIdType.MESH
BLK = 384
STRIP = 128
GROUPS = 8
SLOTS = 5
DIAG, ALONG_X, ALONG_Y, HERE = range(4)
STEPS = 20


def square(rows=STRIP):
    return (lax.broadcasted_iota(jnp.int32, (rows, STRIP), 0), lax.broadcasted_iota(jnp.int32, (rows, STRIP), 1))


FOLD = STRIP // 2
CORNER = FOLD + 8


def pack_left(block):
    row, col = square()
    s11 = block[1, STRIP:2 * STRIP]
    block[0, 0:STRIP] = jnp.where(row >= col, block[0, 0:STRIP], s11)
    block[1, 0:STRIP] = block[1, 2 * STRIP:]
    main = jnp.sum(jnp.where(row == col, s11, 0.0), axis=0, keepdims=True)
    block[2, FOLD:CORNER] = jnp.where(square(8)[0] == 0, main, 0.0)


def pack_corner(block):
    row, col = square(FOLD)
    upper = block[2, 2 * STRIP:2 * STRIP + FOLD]
    lower = block[2, 2 * STRIP + FOLD:]
    main = jnp.sum(jnp.where(row == col, upper, 0.0), axis=0, keepdims=True)
    block[2, 0:FOLD] = jnp.where(col - FOLD > row, pltpu.roll(upper, FOLD, 1), lower)
    block[2, FOLD:CORNER] = jnp.where(square(8)[0] == 1, main, block[2, FOLD:CORNER])


def unpack_symmetric(ref, left, s21, corner):
    row, col = square()
    both, s10, s20 = left[0:STRIP], left[STRIP:2 * STRIP], left[2 * STRIP:]
    both_t = both.T
    fold = corner[0:FOLD]
    low = jnp.concatenate([pltpu.roll(fold, FOLD, 1), fold], axis=0)
    straight = jnp.where(jnp.maximum(row, col) >= FOLD, row - col, col - row) >= 0
    s22 = jnp.where(straight, low, low.T)
    ref[0:STRIP, 0:STRIP] = jnp.where(row >= col, both, both_t)
    ref[STRIP:2 * STRIP, STRIP:2 * STRIP] = jnp.where(
        row == col, corner[FOLD:FOLD + 1], jnp.where(row < col, both, both_t))
    ref[2 * STRIP:, 2 * STRIP:] = jnp.where(
        jnp.logical_and(row == col, row < FOLD), corner[FOLD + 1:FOLD + 2], s22)
    ref[STRIP:2 * STRIP, 0:STRIP] = s10
    ref[0:STRIP, STRIP:2 * STRIP] = s10.T
    ref[2 * STRIP:, 0:STRIP] = s20
    ref[0:STRIP, 2 * STRIP:] = s20.T
    ref[2 * STRIP:, STRIP:2 * STRIP] = s21
    ref[STRIP:2 * STRIP, 2 * STRIP:] = s21.T


def gram_kernel(a_hbm, out_ref, a_buf, acc, stage, mine, from_x, from_y, relay_x, relay_y,
                load_sem, stage_sem, pair_sem, send_sem, fx_sem, fy_sem, rx_sem, ry_sem):
    me = lax.axis_index('dp')
    core = lax.rem(me, 2)
    x = lax.rem(me // 2, 2)
    y = me // 4
    half = a_buf.shape[1] // 2

    def device(xx, yy, kk):
        return (yy * 2 + xx) * 2 + kk

    pair = device(x, y, 1 - core)
    nbr_x = device(1 - x, y, core)
    nbr_y = device(x, 1 - y, core)

    barrier = pltpu.get_barrier_semaphore()
    for other in (pair, nbr_x, nbr_y):
        pl.semaphore_signal(barrier, inc=1, device_id={'dp': other}, device_id_type=MESH)

    far = device(1 - x, 1 - y, 0)

    def load(n, part=None):
        if isinstance(n, int) and n < 2:
            row = far + (1 - core if n == 0 else core)
        else:
            row = lax.rem(far + 1 - n + GROUPS, GROUPS)
        rows = pl.ds(pl.multiple_of(row * BLK, BLK), BLK)
        if part is None:
            return pltpu.make_async_copy(a_hbm.at[rows, :], a_buf.at[rows, :], load_sem.at[n])
        cols = pl.ds(part * half, half)
        return pltpu.make_async_copy(a_hbm.at[rows, cols], a_buf.at[rows, cols], load_sem.at[GROUPS * part])

    load(0, 0).start()
    load(0, 1).start()
    for n in range(1, GROUPS):
        load(n).start()

    near_first = ALONG_X + y
    near_second = ALONG_Y - y

    def step_task(step):
        mid = step - SLOTS
        in_mid = jnp.logical_and(mid >= 0, mid < 2 * SLOTS)
        near = jnp.where(lax.rem(mid + 2 * SLOTS, 2) == 0, near_first, near_second)
        rel = jnp.where(step < SLOTS, DIAG, jnp.where(in_mid, near, HERE))
        slot = jnp.where(step < SLOTS, step, jnp.where(in_mid, mid // 2, step - 3 * SLOTS))
        return rel, slot

    def dest_xy(rel):
        flip_x = jnp.where(rel <= ALONG_X, 1, 0)
        flip_y = jnp.where(lax.rem(rel, 2) == 0, 1, 0)
        xx = x + flip_x - 2 * flip_x * x
        yy = y + flip_y - 2 * flip_y * y
        return xx, yy

    def exists(rel, slot):
        _, yy = dest_xy(rel)
        return jnp.logical_or(slot < SLOTS - 1, yy == 0)

    def dot(lo, lo_rows, hi, hi_rows, cols=slice(None)):
        return lax.dot_general(a_buf[pl.ds(lo, lo_rows), cols], a_buf[pl.ds(hi, hi_rows), cols],
                               (((1,), (1,)), ((), ())), preferred_element_type=jnp.float32)

    def block_rows(rel, slot, kk):
        xx, yy = dest_xy(rel)
        p = device(xx, yy, kk)
        q = lax.rem(p - slot + GROUPS, GROUPS)
        hi = pl.multiple_of(jnp.maximum(p, q) * BLK, BLK)
        lo = pl.multiple_of(jnp.minimum(p, q) * BLK, BLK)
        return hi, lo

    def product(block, hi, lo, first=0, count=3):
        val = dot(hi, BLK, lo + first * STRIP, count * STRIP)
        for m in range(count):
            block[first + m] = val[:, m * STRIP:(m + 1) * STRIP]

    def part(ref, m, first):
        if first and m:
            return ref.at[m, pl.ds(0, STRIP if m == 1 else CORNER)]
        return ref.at[m]

    def pair_copy(rel, slot, src, dst, m=0):
        return pltpu.make_async_remote_copy(
            src_ref=src, dst_ref=dst, send_sem=stage_sem.at[m], recv_sem=pair_sem.at[rel, slot, m],
            device_id={'dp': pair}, device_id_type=MESH)

    def pair_block(rel, slot):
        return pair_copy(rel, slot, stage.at[0], acc.at[rel, slot])

    def by_y(ordinal, dest_x, dest_y):
        later = ordinal - 3
        n, o = 5 - core, 7 + core
        short = (later * 2 + 3) // 3 - (later * 2 + 1) // 3
        full = ((later + 1) * n + o) // 12 - (later * n + o) // 12
        small = jnp.where(jnp.logical_and(dest_x == 1, dest_y == 0), 0, 1 - core)
        early = jnp.where(ordinal == 0, core, small)
        return jnp.where(ordinal < 3, early, jnp.where(dest_y == 1, short, full)) == 1

    def ordinal(slot, m, first):
        return m if first else 3 * slot + m

    def far_send(slot, m, first, along_y):
        return pltpu.make_async_remote_copy(
            src_ref=part(acc.at[DIAG, slot], m, first),
            dst_ref=part((relay_x if along_y else relay_y).at[slot], m, first),
            send_sem=send_sem.at[DIAG, slot, m],
            recv_sem=(rx_sem if along_y else ry_sem).at[slot, m],
            device_id={'dp': nbr_y if along_y else nbr_x}, device_id_type=MESH)

    def near_send(rel, slot, m, first):
        along_y = rel == ALONG_Y
        return pltpu.make_async_remote_copy(
            src_ref=part(acc.at[rel, slot], m, first),
            dst_ref=part((from_y if along_y else from_x).at[slot], m, first),
            send_sem=send_sem.at[rel, slot, m],
            recv_sem=(fy_sem if along_y else fx_sem).at[slot, m],
            device_id={'dp': nbr_y if along_y else nbr_x}, device_id_type=MESH)

    def finish(rel, slot, m, first, only_far=False):
        total = part(acc.at[rel, slot], m, first)
        total[...] = total[...] + part(mine, m, first)[...]

        def send_far():
            along_y = by_y(ordinal(slot, m, first), 1 - x, 1 - y)

            @pl.when(along_y)
            def _():
                far_send(slot, m, first, True).start()

            @pl.when(jnp.logical_not(along_y))
            def _():
                far_send(slot, m, first, False).start()

        if only_far:
            send_far()
            return
        pl.when(rel == DIAG)(send_far)

        @pl.when(rel == ALONG_X)
        def _():
            @pl.when(by_y(ordinal(slot, m, first), 1 - x, y))
            def _():
                far_send(slot, m, first, True).wait_recv()
                total = part(acc.at[ALONG_X, slot], m, first)
                total[...] = total[...] + part(relay_x.at[slot], m, first)[...]

            near_send(ALONG_X, slot, m, first).start()

        @pl.when(rel == ALONG_Y)
        def _():
            @pl.when(jnp.logical_not(by_y(ordinal(slot, m, first), x, 1 - y)))
            def _():
                far_send(slot, m, first, False).wait_recv()
                total = part(acc.at[ALONG_Y, slot], m, first)
                total[...] = total[...] + part(relay_y.at[slot], m, first)[...]

            near_send(ALONG_Y, slot, m, first).start()

    def start_part(slot, m, first):
        copy = pair_copy(DIAG, slot, part(stage.at[slot], m, first), part(acc.at[DIAG, slot], m, first), 3 * slot + m)
        return copy

    def left_product(block, kk, halves):
        row = pl.multiple_of((far + kk) * BLK, BLK)
        for h in range(halves):
            if halves > 1:
                load(0, h).wait()
            cols = pl.ds(h * half, half) if halves > 1 else slice(None)
            val = dot(row, BLK, row, 2 * STRIP, cols)
            for m in range(2):
                now = val[:, m * STRIP:(m + 1) * STRIP]
                block[m] = block[m] + now if h else now
        pack_left(block)

    def corner_product(block, kk):
        row = pl.multiple_of((far + kk) * BLK + 2 * STRIP, STRIP)
        block[2, 2 * STRIP:] = dot(row, STRIP, row, STRIP)
        pack_corner(block)

    def start_finish(slot, parts, first):
        for m in parts:
            start_part(slot, m, first).wait_recv()
            finish(DIAG, slot, m, first, only_far=True)

    left_product(stage.at[0], 1 - core, 2)
    pl.semaphore_wait(barrier, 3)
    start_part(0, 0, True).start()
    start_part(0, 1, True).start()
    load(1).wait()
    left_product(mine, core, 1)
    corner_product(stage.at[0], 1 - core)
    start_part(0, 2, True).start()
    start_finish(0, (0, 1), True)
    corner_product(mine, core)
    load(2).wait()
    product(stage.at[1], *block_rows(DIAG, 1, 1 - core), 0, 2)
    start_part(1, 0, False).start()
    start_part(1, 1, False).start()
    start_finish(0, (2,), True)
    product(mine, *block_rows(DIAG, 1, core), 0, 2)
    product(stage.at[1], *block_rows(DIAG, 1, 1 - core), 2, 1)
    start_part(1, 2, False).start()
    start_finish(1, (0, 1), False)
    product(mine, *block_rows(DIAG, 1, core), 2, 1)
    start_finish(1, (2,), False)
    for m in range(3):
        start_part(0, m, True).wait_send()
        start_part(1, m, False).wait_send()

    def body(step, carry):
        @pl.when(step < SLOTS + 1)
        def _():
            load(step + 1).wait()

        @pl.when(step == SLOTS)
        def _():
            load(GROUPS - 1).wait()

        rel, slot = step_task(step)

        @pl.when(exists(rel, slot))
        def _():
            product(stage.at[0], *block_rows(rel, slot, 1 - core))

            @pl.when(slot == 0)
            def _():
                pack_left(stage.at[0])
                pack_corner(stage.at[0])

            pair_block(rel, slot).start()
            product(mine, *block_rows(rel, slot, core))

            @pl.when(slot == 0)
            def _():
                pack_left(mine)
                pack_corner(mine)
                pair_block(rel, slot).wait_recv()
                for m in range(3):
                    finish(rel, slot, m, True)

            @pl.when(slot > 0)
            def _():
                pair_block(rel, slot).wait_recv()
                for m in range(3):
                    finish(rel, slot, m, False)

            pair_block(rel, slot).wait_send()

        return carry

    lax.fori_loop(2, STEPS, body, 0)

    def arrived(slot, m, first):
        near_send(ALONG_X, slot, m, first).wait_recv()
        near_send(ALONG_Y, slot, m, first).wait_recv()
        return (part(acc.at[HERE, slot], m, first)[...] + part(from_x.at[slot], m, first)[...]
                + part(from_y.at[slot], m, first)[...])

    unpack_symmetric(out_ref.at[0, 0], *(arrived(0, m, True) for m in range(3)))
    for slot in range(1, SLOTS):
        @pl.when(exists(HERE, slot))
        def _(slot=slot):
            for m in range(3):
                out_ref[0, slot, :, m * STRIP:(m + 1) * STRIP] = arrived(slot, m, False)

    @pl.when(jnp.logical_not(exists(HERE, SLOTS - 1)))
    def _():
        out_ref[0, SLOTS - 1] = jnp.zeros((BLK, BLK), jnp.float32)

    for rel in (DIAG, ALONG_X, ALONG_Y):
        for slot in range(SLOTS):
            @pl.when(exists(rel, slot))
            def _(rel=rel, slot=slot):
                for m in range(3):
                    if rel == DIAG:
                        far_send(slot, m, slot == 0, True).wait_send()
                    else:
                        near_send(rel, slot, m, slot == 0).wait_send()


def solution(mesh):
    def local_gram(a_local):
        held = (SLOTS, 3, BLK, STRIP)
        dma = pltpu.SemaphoreType.DMA
        return pl.pallas_call(
            gram_kernel,
            out_shape=pltpu.VMEM((1, SLOTS, BLK, BLK), jnp.float32),
            in_specs=[pl.BlockSpec(memory_space=pl.ANY)],
            out_specs=pl.BlockSpec(memory_space=pltpu.VMEM),
            scratch_shapes=[
                pltpu.VMEM(a_local.shape, a_local.dtype),
                pltpu.VMEM((4,) + held, jnp.float32),
                pltpu.VMEM((2,) + held[1:], jnp.float32),
                pltpu.VMEM(held[1:], jnp.float32),
                pltpu.VMEM(held, jnp.float32),
                pltpu.VMEM(held, jnp.float32),
                pltpu.VMEM(held, jnp.float32),
                pltpu.VMEM(held, jnp.float32),
                dma((GROUPS + 1,)),
                dma((6,)),
                dma((4, SLOTS, 6)),
                dma((3, SLOTS, 3)),
                dma((SLOTS, 3)),
                dma((SLOTS, 3)),
                dma((SLOTS, 3)),
                dma((SLOTS, 3)),
            ],
            compiler_params=pltpu.CompilerParams(
                collective_id=0, has_side_effects=True, vmem_limit_bytes=56623104),
        )(a_local)

    return jax.shard_map(local_gram, mesh=mesh, in_specs=(P('mat', 'dp'),), out_specs=P(('mat', 'dp')), check_vma=False)
```

time: 91.7 us -> 95.1 us (1.037)
  Pallas kernels: 89.3 us -> 93.4 us
    pallas_call x1, Pallas kernels: 89.3 us -> 93.4 us  [local_gram(): pl.pallas_call(gram_kernel, out_shape=pltpu.VMEM((1, SLOTS, BLK, BLK), jn...]
where the time goes in v3:
time: 95.1 us; the launch traced here: 95 us
  Pallas kernels  93.4 us (98%)
  local copies, waits for them, and re-layouts  1.6 us (2%)
    pallas_call x1, Pallas kernels, local_gram(): pl.pallas_call(gram_kernel, out_shape=pltpu.VMEM((1, SLOTS, BLK, BLK), jn...  93.4 us

profile of v3, /device:TPU:0, one launch (start us, length us, event | category | flops | bytes accessed | tf_op | source)
XLA Modules:
  0.0 95.0 jit_solution(17007512711502411259)
XLA Ops:
  0.0 93.4 %shard_map.17 = f32[1,5,384,384]{3,2,1,0:T(8,128)S(1)} custom-call(bf16[3072,4096]{1,0:T(8,128)(2,1)} %a_hbm.1), custom_call_target="tpu_custom_call" | custom-call | tf_op jit(solution)/shard_map/pallas_call | solution.py:350
  93.4 1.6 %copy.3 = f32[1,5,384,384]{3,2,1,0:T(8,128)} copy(f32[1,5,384,384]{3,2,1,0:T(8,128)S(1)} %shard_map.17) | data formatting | bytes 5898240

commit v4 on v3

v4 whole, which is shorter than its diff:
```python
import functools

import jax
import jax.numpy as jnp
from jax import lax
from jax.experimental import pallas as pl
from jax.experimental.pallas import tpu as pltpu
from jax.sharding import PartitionSpec as P

MESH = pl.DeviceIdType.MESH
BLK = 384
STRIP = 128
ROWS = 3 * BLK
GROUPS = 8
SLOTS = 5
DIAG, ALONG_X, ALONG_Y, HERE = range(4)
STEPS = 20


def square(rows=STRIP):
    return (lax.broadcasted_iota(jnp.int32, (rows, STRIP), 0), lax.broadcasted_iota(jnp.int32, (rows, STRIP), 1))


FOLD = STRIP // 2
CORNER = FOLD + 8
FIRST_PARTS = (BLK, STRIP, CORNER)


def rows_of(m, start, stop):
    return slice(m * BLK + start, m * BLK + stop)


def pack_left(block):
    row, col = square()
    s11 = block[rows_of(1, STRIP, 2 * STRIP)]
    block[rows_of(0, 0, STRIP)] = jnp.where(row >= col, block[rows_of(0, 0, STRIP)], s11)
    block[rows_of(1, 0, STRIP)] = block[rows_of(1, 2 * STRIP, BLK)]
    main = jnp.sum(jnp.where(row == col, s11, 0.0), axis=0, keepdims=True)
    block[rows_of(2, FOLD, CORNER)] = jnp.where(square(8)[0] == 0, main, 0.0)


def pack_corner(block):
    row, col = square(FOLD)
    upper = block[rows_of(2, 2 * STRIP, 2 * STRIP + FOLD)]
    lower = block[rows_of(2, 2 * STRIP + FOLD, BLK)]
    main = jnp.sum(jnp.where(row == col, upper, 0.0), axis=0, keepdims=True)
    block[rows_of(2, 0, FOLD)] = jnp.where(col - FOLD > row, pltpu.roll(upper, FOLD, 1), lower)
    block[rows_of(2, FOLD, CORNER)] = jnp.where(square(8)[0] == 1, main, block[rows_of(2, FOLD, CORNER)])


def unpack_symmetric(ref, left, s21, corner):
    row, col = square()
    both, s10, s20 = left[0:STRIP], left[STRIP:2 * STRIP], left[2 * STRIP:]
    both_t = both.T
    fold = corner[0:FOLD]
    low = jnp.concatenate([pltpu.roll(fold, FOLD, 1), fold], axis=0)
    straight = jnp.where(jnp.maximum(row, col) >= FOLD, row - col, col - row) >= 0
    s22 = jnp.where(straight, low, low.T)
    ref[0:STRIP, 0:STRIP] = jnp.where(row >= col, both, both_t)
    ref[STRIP:2 * STRIP, STRIP:2 * STRIP] = jnp.where(
        row == col, corner[FOLD:FOLD + 1], jnp.where(row < col, both, both_t))
    ref[2 * STRIP:, 2 * STRIP:] = jnp.where(
        jnp.logical_and(row == col, row < FOLD), corner[FOLD + 1:FOLD + 2], s22)
    ref[STRIP:2 * STRIP, 0:STRIP] = s10
    ref[0:STRIP, STRIP:2 * STRIP] = s10.T
    ref[2 * STRIP:, 0:STRIP] = s20
    ref[0:STRIP, 2 * STRIP:] = s20.T
    ref[2 * STRIP:, STRIP:2 * STRIP] = s21
    ref[STRIP:2 * STRIP, 2 * STRIP:] = s21.T


def part(block, m, first):
    return block.at[pl.ds(m * BLK, FIRST_PARTS[m] if first else BLK)]


def gram_kernel(a_hbm, out_ref, a_buf, acc, stage, stage_next, mine, from_x, from_y, relay_x, relay_y,
                load_sem, stage_sem, pair_sem, send_sem, fx_sem, fy_sem, rx_sem, ry_sem):
    me = lax.axis_index('dp')
    core = lax.rem(me, 2)
    x = lax.rem(me // 2, 2)
    y = me // 4
    half = a_buf.shape[1] // 2
    one = 1 + me // GROUPS

    def device(xx, yy, kk):
        return (yy * 2 + xx) * 2 + kk

    pair = device(x, y, 1 - core)
    nbr_x = device(1 - x, y, core)
    nbr_y = device(x, 1 - y, core)

    barrier = pltpu.get_barrier_semaphore()
    for other in (pair, nbr_x, nbr_y):
        pl.semaphore_signal(barrier, inc=1, device_id={'dp': other}, device_id_type=MESH)

    far = device(1 - x, 1 - y, 0)

    def load(n):
        row = far + core if isinstance(n, int) and n == 1 else lax.rem(far + 1 - n + GROUPS, GROUPS)
        rows = pl.ds(pl.multiple_of(row * BLK, BLK), BLK)
        return pltpu.make_async_copy(a_hbm.at[rows, :], a_buf.at[rows, :], load_sem.at[n])

    def load_half(h):
        rows = pl.ds(pl.multiple_of((far + 1 - core) * BLK, BLK), BLK)
        cols = pl.ds(pl.multiple_of(h * half, half), half)
        return pltpu.make_async_copy(a_hbm.at[rows, cols], a_buf.at[rows, cols], load_sem.at[GROUPS * h])

    load_half(0).start()
    load_half(1).start()
    for n in range(1, GROUPS):
        load(n).start()

    near_first = ALONG_X + y
    near_second = ALONG_Y - y

    def step_task(step):
        mid = step - SLOTS
        in_mid = jnp.logical_and(mid >= 0, mid < 2 * SLOTS)
        near = jnp.where(lax.rem(mid + 2 * SLOTS, 2) == 0, near_first, near_second)
        rel = jnp.where(step < SLOTS, DIAG, jnp.where(in_mid, near, HERE))
        slot = jnp.where(step < SLOTS, step, jnp.where(in_mid, mid // 2, step - 3 * SLOTS))
        return rel, slot

    def dest_xy(rel):
        flip_x = jnp.where(rel <= ALONG_X, 1, 0)
        flip_y = jnp.where(lax.rem(rel, 2) == 0, 1, 0)
        xx = x + flip_x - 2 * flip_x * x
        yy = y + flip_y - 2 * flip_y * y
        return xx, yy

    def exists(rel, slot):
        _, yy = dest_xy(rel)
        return jnp.logical_or(slot < SLOTS - 1, yy == 0)

    def held(ref, slot):
        return ref.at[pl.ds(pl.multiple_of(slot * ROWS, ROWS), ROWS)]

    def total_of(rel, slot):
        return held(acc, rel * SLOTS + slot)

    def dot(left, left_rows, right, right_rows, cols=slice(None)):
        return lax.dot_general(a_buf[pl.ds(left, left_rows), cols], a_buf[pl.ds(right, right_rows), cols],
                               (((1,), (1,)), ((), ())), preferred_element_type=jnp.float32)

    def block_rows(rel, slot, kk):
        xx, yy = dest_xy(rel)
        p = device(xx, yy, kk)
        q = lax.rem(p - slot + GROUPS, GROUPS)
        hi = pl.multiple_of(jnp.maximum(p, q) * BLK, BLK)
        lo = pl.multiple_of(jnp.minimum(p, q) * BLK, BLK)
        return hi, lo

    def product(block, hi, lo, first=0, count=3):
        val = dot(hi, BLK, lo + first * STRIP, count * STRIP)
        for m in range(count):
            block[rows_of(first + m, 0, BLK)] = val[:, m * STRIP:(m + 1) * STRIP]

    def alone(work):
        def run(_, carry):
            work()
            return carry

        lax.fori_loop(0, one, run, 0)

    def pair_copy(src, dst, send, recv):
        return pltpu.make_async_remote_copy(
            src_ref=src, dst_ref=dst, send_sem=stage_sem.at[send], recv_sem=pair_sem.at[recv],
            device_id={'dp': pair}, device_id_type=MESH)

    def pair_block(step):
        return pair_copy(stage, total_of(*step_task(step)), 0, 5 + lax.rem(step, 3))

    def by_y(ordinal, dest_x, dest_y):
        later = ordinal - 3
        n = jnp.where(dest_x == 1, 4 + core, 5 - core)
        short = (later * 2 + 3) // 3 - (later * 2 + 1) // 3
        full = (later * n + 12) // 12 - (later * n + 12 - n) // 12
        early = jnp.where(ordinal == 0, core, 1 - core)
        return jnp.where(ordinal < 3, early, jnp.where(dest_y == 1, short, full)) == 1

    def ordinal(slot, m, first):
        return m if first else 3 * slot + m

    def far_send(slot, m, first, along_y):
        return pltpu.make_async_remote_copy(
            src_ref=part(total_of(DIAG, slot), m, first),
            dst_ref=part(held(relay_x if along_y else relay_y, slot), m, first),
            send_sem=send_sem.at[DIAG],
            recv_sem=(rx_sem if along_y else ry_sem).at[slot, m],
            device_id={'dp': nbr_y if along_y else nbr_x}, device_id_type=MESH)

    def near_send(rel, slot, m, first):
        along_y = rel == ALONG_Y
        return pltpu.make_async_remote_copy(
            src_ref=part(total_of(rel, slot), m, first),
            dst_ref=part(held(from_y if along_y else from_x, slot), m, first),
            send_sem=send_sem.at[rel],
            recv_sem=(fy_sem if along_y else fx_sem).at[slot],
            device_id={'dp': nbr_y if along_y else nbr_x}, device_id_type=MESH)

    def finish(rel, slot, m, first, only_far=False):
        total = part(total_of(rel, slot), m, first)
        total[...] = total[...] + part(mine, m, first)[...]

        def send_far():
            along_y = by_y(ordinal(slot, m, first), 1 - x, 1 - y)

            @pl.when(along_y)
            def _():
                far_send(slot, m, first, True).start()

            @pl.when(jnp.logical_not(along_y))
            def _():
                far_send(slot, m, first, False).start()

        if only_far:
            send_far()
            return
        pl.when(rel == DIAG)(send_far)

        @pl.when(rel == ALONG_X)
        def _():
            @pl.when(by_y(ordinal(slot, m, first), 1 - x, y))
            def _():
                far_send(slot, m, first, True).wait_recv()
                total = part(total_of(ALONG_X, slot), m, first)
                total[...] = total[...] + part(held(relay_x, slot), m, first)[...]

            near_send(ALONG_X, slot, m, first).start()

        @pl.when(rel == ALONG_Y)
        def _():
            @pl.when(jnp.logical_not(by_y(ordinal(slot, m, first), x, 1 - y)))
            def _():
                far_send(slot, m, first, False).wait_recv()
                total = part(total_of(ALONG_Y, slot), m, first)
                total[...] = total[...] + part(held(relay_y, slot), m, first)[...]

            near_send(ALONG_Y, slot, m, first).start()

    def left_half(block, kk, h):
        row = pl.multiple_of((far + kk) * BLK, BLK)
        val = dot(row, BLK, row, 2 * STRIP, pl.ds(pl.multiple_of(h * half, half), half))
        for m in range(2):
            block[rows_of(m, 0, BLK)] = (
                jnp.where(h > 0, block[rows_of(m, 0, BLK)], 0.0) + val[:, m * STRIP:(m + 1) * STRIP])

    def left_product(block, kk):
        row = pl.multiple_of((far + kk) * BLK, BLK)
        val = dot(row, BLK, row, 2 * STRIP)
        for m in range(2):
            block[rows_of(m, 0, BLK)] = val[:, m * STRIP:(m + 1) * STRIP]

    def corner_product(block, kk):
        row = pl.multiple_of((far + kk) * BLK + 2 * STRIP, STRIP)
        block[rows_of(2, 2 * STRIP, BLK)] = dot(row, STRIP, row, STRIP)

    def first_half(h, carry):
        load_half(h).wait()
        left_half(stage, 1 - core, h)
        return carry

    two = pl.ds(0, 2 * BLK)
    first_total, next_total = total_of(DIAG, 0), total_of(DIAG, 1)
    copies = (
        pair_copy(part(stage, 0, True), part(first_total, 0, True), 0, 0),
        pair_copy(part(stage, 1, True), part(first_total, 1, True), 1, 1),
        pair_copy(part(stage, 2, True), part(first_total, 2, True), 2, 2),
        pair_copy(stage_next.at[two], next_total.at[two], 3, 3),
        pair_copy(part(stage_next, 2, False), part(next_total, 2, False), 4, 4),
    )

    lax.fori_loop(0, 2 * one, first_half, 0)
    pack_left(stage)
    pl.semaphore_wait(barrier, 3)
    copies[0].start()
    copies[1].start()
    load(1).wait()
    alone(lambda: left_product(mine, core))
    pack_left(mine)
    alone(lambda: corner_product(stage, 1 - core))
    pack_corner(stage)
    copies[2].start()
    copies[0].wait_recv()
    finish(DIAG, 0, 0, True, only_far=True)
    copies[1].wait_recv()
    finish(DIAG, 0, 1, True, only_far=True)
    load(2).wait()
    alone(lambda: product(stage_next, *block_rows(DIAG, 1, 1 - core), 0, 2))
    copies[3].start()
    alone(lambda: corner_product(mine, core))
    pack_corner(mine)
    copies[2].wait_recv()
    finish(DIAG, 0, 2, True, only_far=True)
    alone(lambda: product(mine, *block_rows(DIAG, 1, core), 0, 2))
    copies[3].wait_recv()
    finish(DIAG, 1, 0, False, only_far=True)
    finish(DIAG, 1, 1, False, only_far=True)
    alone(lambda: product(stage_next, *block_rows(DIAG, 1, 1 - core), 2, 1))
    copies[4].start()
    alone(lambda: product(mine, *block_rows(DIAG, 1, core), 2, 1))
    copies[4].wait_recv()
    finish(DIAG, 1, 2, False, only_far=True)
    for copy in copies:
        copy.wait_send()

    def body(step, carry):
        @pl.when(step < SLOTS + 1)
        def _():
            load(step + 1).wait()

        @pl.when(step == SLOTS)
        def _():
            load(GROUPS - 1).wait()

        rel, slot = step_task(step)

        @pl.when(exists(rel, slot))
        def _():
            product(stage, *block_rows(rel, slot, 1 - core))

            @pl.when(slot == 0)
            def _():
                pack_left(stage)
                pack_corner(stage)

            pair_block(step).start()
            product(mine, *block_rows(rel, slot, core))

            @pl.when(slot == 0)
            def _():
                pack_left(mine)
                pack_corner(mine)
                pair_block(step).wait_recv()
                for m in range(3):
                    finish(rel, slot, m, True)

            @pl.when(slot > 0)
            def _():
                pair_block(step).wait_recv()
                for m in range(3):
                    finish(rel, slot, m, False)

            pair_block(step).wait_send()

        return carry

    lax.fori_loop(2, STEPS, body, 0)

    def arrived(slot):
        first = slot == 0
        size = pl.ds(0, sum(FIRST_PARTS) if first else ROWS)
        for ref, sem in ((from_x, fx_sem), (from_y, fy_sem)):
            whole = held(ref, slot).at[size]
            pltpu.make_async_copy(whole, whole, sem.at[slot]).wait()
        for m in range(3):
            yield (part(total_of(HERE, slot), m, first)[...] + part(held(from_x, slot), m, first)[...]
                   + part(held(from_y, slot), m, first)[...])

    unpack_symmetric(out_ref.at[0, 0], *arrived(0))
    for slot in range(1, SLOTS):
        @pl.when(exists(HERE, slot))
        def _(slot=slot):
            for m, total in enumerate(arrived(slot)):
                out_ref[0, slot, :, m * STRIP:(m + 1) * STRIP] = total

    @pl.when(jnp.logical_not(exists(HERE, SLOTS - 1)))
    def _():
        out_ref[0, SLOTS - 1] = jnp.zeros((BLK, BLK), jnp.float32)

    for rel in (DIAG, ALONG_X, ALONG_Y):
        for slots in (SLOTS - 1, SLOTS):
            @pl.when(exists(rel, SLOTS - 1) == (slots == SLOTS))
            def _(rel=rel, slots=slots):
                everything = acc.at[pl.ds(0, sum(FIRST_PARTS) + (slots - 1) * ROWS)]
                pltpu.make_async_copy(everything, everything, send_sem.at[rel]).wait()


def solution(mesh):
    def local_gram(a_local):
        dma = pltpu.SemaphoreType.DMA

        def blocks(n):
            return pltpu.VMEM((n * ROWS, STRIP), jnp.float32)

        return pl.pallas_call(
            gram_kernel,
            out_shape=pltpu.VMEM((1, SLOTS, BLK, BLK), jnp.float32),
            in_specs=[pl.BlockSpec(memory_space=pl.ANY)],
            out_specs=pl.BlockSpec(memory_space=pltpu.VMEM),
            scratch_shapes=[
                pltpu.VMEM(a_local.shape, a_local.dtype),
                blocks(4 * SLOTS), blocks(1), blocks(1), blocks(1),
                blocks(SLOTS), blocks(SLOTS), blocks(SLOTS), blocks(SLOTS),
                dma((GROUPS + 1,)), dma((5,)), dma((8,)), dma((3,)),
                dma((SLOTS,)), dma((SLOTS,)), dma((SLOTS, 3)), dma((SLOTS, 3)),
            ],
            compiler_params=pltpu.CompilerParams(
                collective_id=0, has_side_effects=True, vmem_limit_bytes=56623104),
        )(a_local)

    return jax.shard_map(local_gram, mesh=mesh, in_specs=(P('mat', 'dp'),), out_specs=P(('mat', 'dp')), check_vma=False)
```

time: 95.1 us -> 90.5 us (0.952)
  Pallas kernels: 93.4 us -> 88.3 us
    pallas_call x1, Pallas kernels: 93.4 us -> 88.3 us  [local_gram(): pl.pallas_call(gram_kernel, out_shape=pltpu.VMEM((1, SLOTS, BLK, BLK), jn...]
where the time goes in v4:
time: 90.5 us; the launch traced here: 89.9 us
  Pallas kernels  88.3 us (98%)
  local copies, waits for them, and re-layouts  1.6 us (2%)
    pallas_call x1, Pallas kernels, local_gram(): pl.pallas_call(gram_kernel, out_shape=pltpu.VMEM((1, SLOTS, BLK, BLK), jn...  88.3 us

profile of v4, /device:TPU:0, one launch (start us, length us, event | category | flops | bytes accessed | tf_op | source)
XLA Modules:
  0.0 89.9 jit_solution(14415694003944855104)
XLA Ops:
  0.0 88.3 %shard_map.17 = f32[1,5,384,384]{3,2,1,0:T(8,128)S(1)} custom-call(bf16[3072,4096]{1,0:T(8,128)(2,1)} %a_hbm.1), custom_call_target="tpu_custom_call" | custom-call | tf_op jit(solution)/shard_map/pallas_call | solution.py:386
  88.3 1.6 %copy.3 = f32[1,5,384,384]{3,2,1,0:T(8,128)} copy(f32[1,5,384,384]{3,2,1,0:T(8,128)S(1)} %shard_map.17) | data formatting | bytes 5898240

commit v5 on v4

--- a/solution.py
+++ b/solution.py
@@ -14,7 +14,7 @@
 GROUPS = 8
 SLOTS = 5
 DIAG, ALONG_X, ALONG_Y, HERE = range(4)
-STEPS = 20
+STEPS = 4 * SLOTS - 1
 
 
 def square(rows=STRIP):
@@ -23,7 +23,9 @@
 
 FOLD = STRIP // 2
 CORNER = FOLD + 8
-FIRST_PARTS = (BLK, STRIP, CORNER)
+FIRST_PARTS = ((0, BLK), (BLK, STRIP), (2 * BLK, CORNER))
+HALF_PIECE = BLK // 2
+PARTS = ((0, BLK), (BLK, BLK), (2 * BLK, HALF_PIECE), (2 * BLK + HALF_PIECE, HALF_PIECE))
 
 
 def rows_of(m, start, stop):
@@ -70,7 +72,15 @@
 
 
 def part(block, m, first):
-    return block.at[pl.ds(m * BLK, FIRST_PARTS[m] if first else BLK)]
+    return block.at[pl.ds(*(FIRST_PARTS if first else PARTS)[m])]
+
+
+def parts(first):
+    return range(len(FIRST_PARTS if first else PARTS))
+
+
+def size(first):
+    return sum(rows for _, rows in FIRST_PARTS) if first else ROWS
 
 
 def gram_kernel(a_hbm, out_ref, a_buf, acc, stage, stage_next, mine, from_x, from_y, relay_x, relay_y,
@@ -115,10 +125,12 @@
 
     def step_task(step):
         mid = step - SLOTS
-        in_mid = jnp.logical_and(mid >= 0, mid < 2 * SLOTS)
-        near = jnp.where(lax.rem(mid + 2 * SLOTS, 2) == 0, near_first, near_second)
+        in_mid = jnp.logical_and(mid >= 0, mid < 2 * SLOTS - 1)
+        to_first = jnp.logical_or(mid <= 0, lax.rem(mid + 2 * SLOTS, 2) == 1)
+        near = jnp.where(to_first, near_first, near_second)
+        near_slot = jnp.where(to_first, (mid + 1) // 2, mid // 2 - 1)
         rel = jnp.where(step < SLOTS, DIAG, jnp.where(in_mid, near, HERE))
-        slot = jnp.where(step < SLOTS, step, jnp.where(in_mid, mid // 2, step - 3 * SLOTS))
+        slot = jnp.where(step < SLOTS, step, jnp.where(in_mid, near_slot, step - 3 * SLOTS + 1))
         return rel, slot
 
     def dest_xy(rel):
@@ -170,23 +182,34 @@
     def pair_block(step):
         return pair_copy(stage, total_of(*step_task(step)), 0, 5 + lax.rem(step, 3))
 
-    def by_y(ordinal, dest_x, dest_y):
-        later = ordinal - 3
-        n = jnp.where(dest_x == 1, 4 + core, 5 - core)
-        short = (later * 2 + 3) // 3 - (later * 2 + 1) // 3
-        full = (later * n + 12) // 12 - (later * n + 12 - n) // 12
-        early = jnp.where(ordinal == 0, core, 1 - core)
-        return jnp.where(ordinal < 3, early, jnp.where(dest_y == 1, short, full)) == 1
-
-    def ordinal(slot, m, first):
-        return m if first else 3 * slot + m
+    def by_y(slot, m, first, dest_x, dest_y):
+        if first:
+            return (core if m == 0 else 1 - core) == 1
+
+        def listed(*bits):
+            return jnp.where(slot == 1, bits[0], jnp.where(slot == 2, bits[1], jnp.where(slot == 3, bits[2], bits[3])))
+
+        to_zero = jnp.where(core == 0, listed(13, 2, 1, 1), listed(1, 1, 2, 2))
+        to_one = jnp.where(core == 0, listed(5, 2, 1, 1), listed(5, 1, 2, 4))
+        bits = jnp.where(dest_y == 1, 13, jnp.where(dest_x == 0, to_zero, to_one))
+        return lax.rem(bits // 2 ** m, 2) == 1
+
+    def relay_wait(slot, first, relay, sem, flags):
+        rows = sum(jnp.where(flag, part_rows, 0)
+                   for flag, (_, part_rows) in zip(flags, FIRST_PARTS if first else PARTS))
+        possible = (BLK, size(True) - BLK) if first else range(HALF_PIECE, ROWS + 1, HALF_PIECE)
+        for count in possible:
+            @pl.when(rows == count)
+            def _(count=count):
+                whole = held(relay, slot).at[pl.ds(0, count)]
+                pltpu.make_async_copy(whole, whole, sem.at[slot]).wait()
 
     def far_send(slot, m, first, along_y):
         return pltpu.make_async_remote_copy(
             src_ref=part(total_of(DIAG, slot), m, first),
             dst_ref=part(held(relay_x if along_y else relay_y, slot), m, first),
             send_sem=send_sem.at[DIAG],
-            recv_sem=(rx_sem if along_y else ry_sem).at[slot, m],
+            recv_sem=(rx_sem if along_y else ry_sem).at[slot],
             device_id={'dp': nbr_y if along_y else nbr_x}, device_id_type=MESH)
 
     def near_send(rel, slot, m, first):
@@ -198,45 +221,56 @@
             recv_sem=(fy_sem if along_y else fx_sem).at[slot],
             device_id={'dp': nbr_y if along_y else nbr_x}, device_id_type=MESH)
 
-    def finish(rel, slot, m, first, only_far=False):
-        total = part(total_of(rel, slot), m, first)
+    def finish_far(slot, m, first):
+        total = part(total_of(DIAG, slot), m, first)
         total[...] = total[...] + part(mine, m, first)[...]
-
-        def send_far():
-            along_y = by_y(ordinal(slot, m, first), 1 - x, 1 - y)
-
-            @pl.when(along_y)
-            def _():
-                far_send(slot, m, first, True).start()
-
-            @pl.when(jnp.logical_not(along_y))
-            def _():
-                far_send(slot, m, first, False).start()
-
-        if only_far:
-            send_far()
-            return
-        pl.when(rel == DIAG)(send_far)
-
-        @pl.when(rel == ALONG_X)
-        def _():
-            @pl.when(by_y(ordinal(slot, m, first), 1 - x, y))
-            def _():
-                far_send(slot, m, first, True).wait_recv()
-                total = part(total_of(ALONG_X, slot), m, first)
-                total[...] = total[...] + part(held(relay_x, slot), m, first)[...]
-
-            near_send(ALONG_X, slot, m, first).start()
-
-        @pl.when(rel == ALONG_Y)
-        def _():
-            @pl.when(jnp.logical_not(by_y(ordinal(slot, m, first), x, 1 - y)))
-            def _():
-                far_send(slot, m, first, False).wait_recv()
-                total = part(total_of(ALONG_Y, slot), m, first)
-                total[...] = total[...] + part(held(relay_y, slot), m, first)[...]
-
-            near_send(ALONG_Y, slot, m, first).start()
+        along_y = by_y(slot, m, first, 1 - x, 1 - y)
+
+        @pl.when(along_y)
+        def _():
+            far_send(slot, m, first, True).start()
+
+        @pl.when(jnp.logical_not(along_y))
+        def _():
+            far_send(slot, m, first, False).start()
+
+    def finish_near(rel, slot, first):
+        if rel == ALONG_X:
+            relay, sem = relay_x, rx_sem
+            flags = [by_y(slot, m, first, 1 - x, y) for m in parts(first)]
+        else:
+            relay, sem = relay_y, ry_sem
+            flags = [jnp.logical_not(by_y(slot, m, first, x, 1 - y)) for m in parts(first)]
+        relay_wait(slot, first, relay, sem, flags)
+        for m in parts(first):
+            total = part(total_of(rel, slot), m, first)
+
+            @pl.when(flags[m])
+            def _(m=m, total=total):
+                total[...] = total[...] + part(mine, m, first)[...] + part(held(relay, slot), m, first)[...]
+
+            @pl.when(jnp.logical_not(flags[m]))
+            def _(m=m, total=total):
+                total[...] = total[...] + part(mine, m, first)[...]
+
+            near_send(rel, slot, m, first).start()
+
+    def finish(rel, slot, first):
+        @pl.when(rel == DIAG)
+        def _():
+            for m in parts(first):
+                finish_far(slot, m, first)
+
+        for near in (ALONG_X, ALONG_Y):
+            @pl.when(rel == near)
+            def _(near=near):
+                finish_near(near, slot, first)
+
+        @pl.when(rel == HERE)
+        def _():
+            for m in parts(first):
+                total = part(total_of(HERE, slot), m, first)
+                total[...] = total[...] + part(mine, m, first)[...]
 
     def left_half(block, kk, h):
         row = pl.multiple_of((far + kk) * BLK, BLK)
@@ -260,14 +294,14 @@
         left_half(stage, 1 - core, h)
         return carry
 
-    two = pl.ds(0, 2 * BLK)
+    two, last = pl.ds(0, 2 * BLK), pl.ds(2 * BLK, BLK)
     first_total, next_total = total_of(DIAG, 0), total_of(DIAG, 1)
     copies = (
         pair_copy(part(stage, 0, True), part(first_total, 0, True), 0, 0),
         pair_copy(part(stage, 1, True), part(first_total, 1, True), 1, 1),
         pair_copy(part(stage, 2, True), part(first_total, 2, True), 2, 2),
         pair_copy(stage_next.at[two], next_total.at[two], 3, 3),
-        pair_copy(part(stage_next, 2, False), part(next_total, 2, False), 4, 4),
+        pair_copy(stage_next.at[last], next_total.at[last], 4, 4),
     )
 
     lax.fori_loop(0, 2 * one, first_half, 0)
@@ -278,29 +312,30 @@
     load(1).wait()
     alone(lambda: left_product(mine, core))
     pack_left(mine)
+    copies[0].wait_recv()
+    finish_far(0, 0, True)
+    copies[1].wait_recv()
+    finish_far(0, 1, True)
     alone(lambda: corner_product(stage, 1 - core))
     pack_corner(stage)
     copies[2].start()
-    copies[0].wait_recv()
-    finish(DIAG, 0, 0, True, only_far=True)
-    copies[1].wait_recv()
-    finish(DIAG, 0, 1, True, only_far=True)
     load(2).wait()
     alone(lambda: product(stage_next, *block_rows(DIAG, 1, 1 - core), 0, 2))
     copies[3].start()
     alone(lambda: corner_product(mine, core))
     pack_corner(mine)
     copies[2].wait_recv()
-    finish(DIAG, 0, 2, True, only_far=True)
+    finish_far(0, 2, True)
     alone(lambda: product(mine, *block_rows(DIAG, 1, core), 0, 2))
     copies[3].wait_recv()
-    finish(DIAG, 1, 0, False, only_far=True)
-    finish(DIAG, 1, 1, False, only_far=True)
+    finish_far(1, 0, False)
+    finish_far(1, 1, False)
     alone(lambda: product(stage_next, *block_rows(DIAG, 1, 1 - core), 2, 1))
     copies[4].start()
     alone(lambda: product(mine, *block_rows(DIAG, 1, core), 2, 1))
     copies[4].wait_recv()
-    finish(DIAG, 1, 2, False, only_far=True)
+    finish_far(1, 2, False)
+    finish_far(1, 3, False)
     for copy in copies:
         copy.wait_send()
 
@@ -332,14 +367,12 @@
                 pack_left(mine)
                 pack_corner(mine)
                 pair_block(step).wait_recv()
-                for m in range(3):
-                    finish(rel, slot, m, True)
+                finish(rel, slot, True)
 
             @pl.when(slot > 0)
             def _():
                 pair_block(step).wait_recv()
-                for m in range(3):
-                    finish(rel, slot, m, False)
+                finish(rel, slot, False)
 
             pair_block(step).wait_send()
 
@@ -349,13 +382,12 @@
 
     def arrived(slot):
         first = slot == 0
-        size = pl.ds(0, sum(FIRST_PARTS) if first else ROWS)
         for ref, sem in ((from_x, fx_sem), (from_y, fy_sem)):
-            whole = held(ref, slot).at[size]
+            whole = held(ref, slot).at[pl.ds(0, size(first))]
             pltpu.make_async_copy(whole, whole, sem.at[slot]).wait()
         for m in range(3):
-            yield (part(total_of(HERE, slot), m, first)[...] + part(held(from_x, slot), m, first)[...]
-                   + part(held(from_y, slot), m, first)[...])
+            rows = pl.ds(*FIRST_PARTS[m]) if first else pl.ds(m * BLK, BLK)
+            yield held(from_x, slot)[rows] + held(from_y, slot)[rows] + total_of(HERE, slot)[rows]
 
     unpack_symmetric(out_ref.at[0, 0], *arrived(0))
     for slot in range(1, SLOTS):
@@ -372,7 +404,7 @@
         for slots in (SLOTS - 1, SLOTS):
             @pl.when(exists(rel, SLOTS - 1) == (slots == SLOTS))
             def _(rel=rel, slots=slots):
-                everything = acc.at[pl.ds(0, sum(FIRST_PARTS) + (slots - 1) * ROWS)]
+                everything = acc.at[pl.ds(0, size(True) + (slots - 1) * ROWS)]
                 pltpu.make_async_copy(everything, everything, send_sem.at[rel]).wait()
 
 
@@ -393,7 +425,7 @@
                 blocks(4 * SLOTS), blocks(1), blocks(1), blocks(1),
                 blocks(SLOTS), blocks(SLOTS), blocks(SLOTS), blocks(SLOTS),
                 dma((GROUPS + 1,)), dma((5,)), dma((8,)), dma((3,)),
-                dma((SLOTS,)), dma((SLOTS,)), dma((SLOTS, 3)), dma((SLOTS, 3)),
+                dma((SLOTS,)), dma((SLOTS,)), dma((SLOTS,)), dma((SLOTS,)),
             ],
             compiler_params=pltpu.CompilerParams(
                 collective_id=0, has_side_effects=True, vmem_limit_bytes=56623104),

time: 90.5 us -> 88.6 us (0.979)
  Pallas kernels: 88.3 us -> 86.9 us
    pallas_call x1, Pallas kernels: 88.3 us -> 86.9 us  [local_gram(): pl.pallas_call(gram_kernel, out_shape=pltpu.VMEM((1, SLOTS, BLK, BLK), jn...]
where the time goes in v5:
time: 88.6 us; the launch traced here: 88.5 us
  Pallas kernels  86.9 us (98%)
  local copies, waits for them, and re-layouts  1.6 us (2%)
    pallas_call x1, Pallas kernels, local_gram(): pl.pallas_call(gram_kernel, out_shape=pltpu.VMEM((1, SLOTS, BLK, BLK), jn...  86.9 us

profile of v5, /device:TPU:0, one launch (start us, length us, event | category | flops | bytes accessed | tf_op | source)
XLA Modules:
  0.0 88.5 jit_solution(6979443018981866107)
XLA Ops:
  0.0 86.9 %shard_map.17 = f32[1,5,384,384]{3,2,1,0:T(8,128)S(1)} custom-call(bf16[3072,4096]{1,0:T(8,128)(2,1)} %a_hbm.1), custom_call_target="tpu_custom_call" | custom-call | tf_op jit(solution)/shard_map/pallas_call | solution.py:418
  86.9 1.6 %copy.3 = f32[1,5,384,384]{3,2,1,0:T(8,128)} copy(f32[1,5,384,384]{3,2,1,0:T(8,128)S(1)} %shard_map.17) | data formatting | bytes 5898240

commit v6 on v5

--- a/solution.py
+++ b/solution.py
@@ -1,4 +1,4 @@
-import functools
+import itertools
 
 import jax
 import jax.numpy as jnp
@@ -24,8 +24,8 @@
 FOLD = STRIP // 2
 CORNER = FOLD + 8
 FIRST_PARTS = ((0, BLK), (BLK, STRIP), (2 * BLK, CORNER))
-HALF_PIECE = BLK // 2
-PARTS = ((0, BLK), (BLK, BLK), (2 * BLK, HALF_PIECE), (2 * BLK + HALF_PIECE, HALF_PIECE))
+CUT = 176
+PARTS = ((0, BLK), (BLK, BLK), (2 * BLK, CUT), (2 * BLK + CUT, BLK - CUT))
 
 
 def rows_of(m, start, stop):
@@ -190,15 +190,15 @@
             return jnp.where(slot == 1, bits[0], jnp.where(slot == 2, bits[1], jnp.where(slot == 3, bits[2], bits[3])))
 
         to_zero = jnp.where(core == 0, listed(13, 2, 1, 1), listed(1, 1, 2, 2))
-        to_one = jnp.where(core == 0, listed(5, 2, 1, 1), listed(5, 1, 2, 4))
+        to_one = jnp.where(core == 0, listed(5, 2, 1, 4), listed(5, 1, 2, 2))
         bits = jnp.where(dest_y == 1, 13, jnp.where(dest_x == 0, to_zero, to_one))
         return lax.rem(bits // 2 ** m, 2) == 1
 
     def relay_wait(slot, first, relay, sem, flags):
-        rows = sum(jnp.where(flag, part_rows, 0)
-                   for flag, (_, part_rows) in zip(flags, FIRST_PARTS if first else PARTS))
-        possible = (BLK, size(True) - BLK) if first else range(HALF_PIECE, ROWS + 1, HALF_PIECE)
-        for count in possible:
+        each = [part_rows for _, part_rows in (FIRST_PARTS if first else PARTS)]
+        rows = sum(jnp.where(flag, part_rows, 0) for flag, part_rows in zip(flags, each))
+        possible = {sum(chosen) for n in range(1, len(each) + 1) for chosen in itertools.combinations(each, n)}
+        for count in sorted(possible):
             @pl.when(rows == count)
             def _(count=count):
                 whole = held(relay, slot).at[pl.ds(0, count)]

time: 88.6 us -> 88.3 us (level)
  no operation moved by 1% of the time
where the time goes in v6:
time: 88.3 us
  Pallas kernels  86.7 us (98%)
  local copies, waits for them, and re-layouts  1.6 us (2%)
    pallas_call x1, Pallas kernels, local_gram(): pl.pallas_call(gram_kernel, out_shape=pltpu.VMEM((1, SLOTS, BLK, BLK), jn...  86.7 us

profile of v6, /device:TPU:0, one launch (start us, length us, event | category | flops | bytes accessed | tf_op | source)
XLA Modules:
  0.0 88.3 jit_solution(15271730666891866962)
XLA Ops:
  0.0 86.7 %shard_map.17 = f32[1,5,384,384]{3,2,1,0:T(8,128)S(1)} custom-call(bf16[3072,4096]{1,0:T(8,128)(2,1)} %a_hbm.1), custom_call_target="tpu_custom_call" | custom-call | tf_op jit(solution)/shard_map/pallas_call | solution.py:418
  86.7 1.6 %copy.3 = f32[1,5,384,384]{3,2,1,0:T(8,128)} copy(f32[1,5,384,384]{3,2,1,0:T(8,128)S(1)} %shard_map.17) | data formatting | bytes 5898240

commit v7 on v6

--- a/solution.py
+++ b/solution.py
@@ -84,7 +84,7 @@
 
 
 def gram_kernel(a_hbm, out_ref, a_buf, acc, stage, stage_next, mine, from_x, from_y, relay_x, relay_y,
-                load_sem, stage_sem, pair_sem, send_sem, fx_sem, fy_sem, rx_sem, ry_sem):
+                load_sem, stage_sem, pair_sem, send_sem, from_sem, rx_sem, ry_sem):
     me = lax.axis_index('dp')
     core = lax.rem(me, 2)
     x = lax.rem(me // 2, 2)
@@ -106,14 +106,14 @@
     far = device(1 - x, 1 - y, 0)
 
     def load(n):
-        row = far + core if isinstance(n, int) and n == 1 else lax.rem(far + 1 - n + GROUPS, GROUPS)
+        row = far + core if n == 1 else lax.rem(far + 1 - n + GROUPS, GROUPS)
         rows = pl.ds(pl.multiple_of(row * BLK, BLK), BLK)
-        return pltpu.make_async_copy(a_hbm.at[rows, :], a_buf.at[rows, :], load_sem.at[n])
+        return pltpu.make_async_copy(a_hbm.at[rows, :], a_buf.at[rows, :], load_sem.at[min(n, 3)])
 
     def load_half(h):
         rows = pl.ds(pl.multiple_of((far + 1 - core) * BLK, BLK), BLK)
         cols = pl.ds(pl.multiple_of(h * half, half), half)
-        return pltpu.make_async_copy(a_hbm.at[rows, cols], a_buf.at[rows, cols], load_sem.at[GROUPS * h])
+        return pltpu.make_async_copy(a_hbm.at[rows, cols], a_buf.at[rows, cols], load_sem.at[4 * h])
 
     load_half(0).start()
     load_half(1).start()
@@ -174,13 +174,13 @@
 
         lax.fori_loop(0, one, run, 0)
 
-    def pair_copy(src, dst, send, recv):
+    def pair_copy(src, dst, recv):
         return pltpu.make_async_remote_copy(
-            src_ref=src, dst_ref=dst, send_sem=stage_sem.at[send], recv_sem=pair_sem.at[recv],
+            src_ref=src, dst_ref=dst, send_sem=stage_sem, recv_sem=pair_sem.at[recv],
             device_id={'dp': pair}, device_id_type=MESH)
 
     def pair_block(step):
-        return pair_copy(stage, total_of(*step_task(step)), 0, 5 + lax.rem(step, 3))
+        return pair_copy(stage, total_of(*step_task(step)), 3 + lax.rem(step + 1, 3))
 
     def by_y(slot, m, first, dest_x, dest_y):
         if first:
@@ -208,7 +208,7 @@
         return pltpu.make_async_remote_copy(
             src_ref=part(total_of(DIAG, slot), m, first),
             dst_ref=part(held(relay_x if along_y else relay_y, slot), m, first),
-            send_sem=send_sem.at[DIAG],
+            send_sem=send_sem,
             recv_sem=(rx_sem if along_y else ry_sem).at[slot],
             device_id={'dp': nbr_y if along_y else nbr_x}, device_id_type=MESH)
 
@@ -217,8 +217,8 @@
         return pltpu.make_async_remote_copy(
             src_ref=part(total_of(rel, slot), m, first),
             dst_ref=part(held(from_y if along_y else from_x, slot), m, first),
-            send_sem=send_sem.at[rel],
-            recv_sem=(fy_sem if along_y else fx_sem).at[slot],
+            send_sem=send_sem,
+            recv_sem=from_sem.at[slot],
             device_id={'dp': nbr_y if along_y else nbr_x}, device_id_type=MESH)
 
     def finish_far(slot, m, first):
@@ -297,11 +297,11 @@
     two, last = pl.ds(0, 2 * BLK), pl.ds(2 * BLK, BLK)
     first_total, next_total = total_of(DIAG, 0), total_of(DIAG, 1)
     copies = (
-        pair_copy(part(stage, 0, True), part(first_total, 0, True), 0, 0),
-        pair_copy(part(stage, 1, True), part(first_total, 1, True), 1, 1),
-        pair_copy(part(stage, 2, True), part(first_total, 2, True), 2, 2),
-        pair_copy(stage_next.at[two], next_total.at[two], 3, 3),
-        pair_copy(stage_next.at[last], next_total.at[last], 4, 4),
+        pair_copy(part(stage, 0, True), part(first_total, 0, True), 0),
+        pair_copy(part(stage, 1, True), part(first_total, 1, True), 1),
+        pair_copy(part(stage, 2, True), part(first_total, 2, True), 2),
+        pair_copy(stage_next.at[two], next_total.at[two], 4),
+        pair_copy(stage_next.at[last], next_total.at[last], 5),
     )
 
     lax.fori_loop(0, 2 * one, first_half, 0)
@@ -336,17 +336,14 @@
     copies[4].wait_recv()
     finish_far(1, 2, False)
     finish_far(1, 3, False)
-    for copy in copies:
-        copy.wait_send()
+    both = acc.at[pl.ds(0, size(True) + ROWS)]
+    pltpu.make_async_copy(both, both, stage_sem).wait()
 
     def body(step, carry):
-        @pl.when(step < SLOTS + 1)
-        def _():
-            load(step + 1).wait()
-
-        @pl.when(step == SLOTS)
-        def _():
-            load(GROUPS - 1).wait()
+        @pl.when(step == 2)
+        def _():
+            rest = pl.ds(0, (GROUPS - 3) * BLK)
+            pltpu.make_async_copy(a_hbm.at[rest, :], a_buf.at[rest, :], load_sem.at[3]).wait()
 
         rel, slot = step_task(step)
 
@@ -382,9 +379,8 @@
 
     def arrived(slot):
         first = slot == 0
-        for ref, sem in ((from_x, fx_sem), (from_y, fy_sem)):
-            whole = held(ref, slot).at[pl.ds(0, size(first))]
-            pltpu.make_async_copy(whole, whole, sem.at[slot]).wait()
+        two_of = acc.at[pl.ds(0, 2 * size(first))]
+        pltpu.make_async_copy(two_of, two_of, from_sem.at[slot]).wait()
         for m in range(3):
             rows = pl.ds(*FIRST_PARTS[m]) if first else pl.ds(m * BLK, BLK)
             yield held(from_x, slot)[rows] + held(from_y, slot)[rows] + total_of(HERE, slot)[rows]
@@ -400,12 +396,11 @@
     def _():
         out_ref[0, SLOTS - 1] = jnp.zeros((BLK, BLK), jnp.float32)
 
-    for rel in (DIAG, ALONG_X, ALONG_Y):
-        for slots in (SLOTS - 1, SLOTS):
-            @pl.when(exists(rel, SLOTS - 1) == (slots == SLOTS))
-            def _(rel=rel, slots=slots):
-                everything = acc.at[pl.ds(0, size(True) + (slots - 1) * ROWS)]
-                pltpu.make_async_copy(everything, everything, send_sem.at[rel]).wait()
+    for longer in (1, 2):
+        @pl.when(y == longer - 1)
+        def _(longer=longer):
+            everything = acc.at[pl.ds(0, 3 * size(True) + (3 * (SLOTS - 2) + longer) * ROWS)]
+            pltpu.make_async_copy(everything, everything, send_sem).wait()
 
 
 def solution(mesh):
@@ -424,8 +419,7 @@
                 pltpu.VMEM(a_local.shape, a_local.dtype),
                 blocks(4 * SLOTS), blocks(1), blocks(1), blocks(1),
                 blocks(SLOTS), blocks(SLOTS), blocks(SLOTS), blocks(SLOTS),
-                dma((GROUPS + 1,)), dma((5,)), dma((8,)), dma((3,)),
-                dma((SLOTS,)), dma((SLOTS,)), dma((SLOTS,)), dma((SLOTS,)),
+                dma((5,)), dma, dma((6,)), dma, dma((SLOTS,)), dma((SLOTS,)), dma((SLOTS,)),
             ],
             compiler_params=pltpu.CompilerParams(
                 collective_id=0, has_side_effects=True, vmem_limit_bytes=56623104),

time: 88.3 us -> 88.2 us (level)
  no operation moved by 1% of the time
where the time goes in v7:
time: 88.2 us; the launch traced here: 88.1 us
  Pallas kernels  86.5 us (98%)
  local copies, waits for them, and re-layouts  1.6 us (2%)
    pallas_call x1, Pallas kernels, local_gram(): pl.pallas_call(gram_kernel, out_shape=pltpu.VMEM((1, SLOTS, BLK, BLK), jn...  86.5 us

profile of v7, /device:TPU:0, one launch (start us, length us, event | category | flops | bytes accessed | tf_op | source)
XLA Modules:
  0.0 88.1 jit_solution(7858553362246103241)
XLA Ops:
  0.0 86.5 %shard_map.17 = f32[1,5,384,384]{3,2,1,0:T(8,128)S(1)} custom-call(bf16[3072,4096]{1,0:T(8,128)(2,1)} %a_hbm.1), custom_call_target="tpu_custom_call" | custom-call | tf_op jit(solution)/shard_map/pallas_call | solution.py:413
  86.5 1.6 %copy.3 = f32[1,5,384,384]{3,2,1,0:T(8,128)} copy(f32[1,5,384,384]{3,2,1,0:T(8,128)S(1)} %shard_map.17) | data formatting | bytes 5898240

commit v8 on v7

--- a/solution.py
+++ b/solution.py
@@ -218,7 +218,7 @@
             src_ref=part(total_of(rel, slot), m, first),
             dst_ref=part(held(from_y if along_y else from_x, slot), m, first),
             send_sem=send_sem,
-            recv_sem=from_sem.at[slot],
+            recv_sem=from_sem.at[slot + jnp.where(slot == SLOTS - 1, m, 0)],
             device_id={'dp': nbr_y if along_y else nbr_x}, device_id_type=MESH)
 
     def finish_far(slot, m, first):
@@ -386,11 +386,21 @@
             yield held(from_x, slot)[rows] + held(from_y, slot)[rows] + total_of(HERE, slot)[rows]
 
     unpack_symmetric(out_ref.at[0, 0], *arrived(0))
-    for slot in range(1, SLOTS):
+    for slot in range(1, SLOTS - 1):
         @pl.when(exists(HERE, slot))
         def _(slot=slot):
             for m, total in enumerate(arrived(slot)):
                 out_ref[0, slot, :, m * STRIP:(m + 1) * STRIP] = total
+
+    @pl.when(exists(HERE, SLOTS - 1))
+    def _():
+        for m, (start, count) in enumerate(PARTS):
+            two_of = acc.at[pl.ds(0, 2 * count)]
+            pltpu.make_async_copy(two_of, two_of, from_sem.at[SLOTS - 1 + m]).wait()
+            rows = pl.ds(start, count)
+            column, row = start // BLK, start % BLK
+            out_ref[0, SLOTS - 1, row:row + count, column * STRIP:(column + 1) * STRIP] = (
+                held(from_x, SLOTS - 1)[rows] + held(from_y, SLOTS - 1)[rows] + total_of(HERE, SLOTS - 1)[rows])
 
     @pl.when(jnp.logical_not(exists(HERE, SLOTS - 1)))
     def _():
@@ -419,7 +429,7 @@
                 pltpu.VMEM(a_local.shape, a_local.dtype),
                 blocks(4 * SLOTS), blocks(1), blocks(1), blocks(1),
                 blocks(SLOTS), blocks(SLOTS), blocks(SLOTS), blocks(SLOTS),
-                dma((5,)), dma, dma((6,)), dma, dma((SLOTS,)), dma((SLOTS,)), dma((SLOTS,)),
+                dma((5,)), dma, dma((6,)), dma, dma((SLOTS + 3,)), dma((SLOTS,)), dma((SLOTS,)),
             ],
             compiler_params=pltpu.CompilerParams(
                 collective_id=0, has_side_effects=True, vmem_limit_bytes=56623104),

time: 88.2 us -> 88.1 us (level)
  no operation moved by 1% of the time
where the time goes in v8:
time: 88.1 us
  Pallas kernels  86.5 us (98%)
  local copies, waits for them, and re-layouts  1.6 us (2%)
    pallas_call x1, Pallas kernels, local_gram(): pl.pallas_call(gram_kernel, out_shape=pltpu.VMEM((1, SLOTS, BLK, BLK), jn...  86.5 us

profile of v8, /device:TPU:0, one launch (start us, length us, event | category | flops | bytes accessed | tf_op | source)
XLA Modules:
  0.0 88.1 jit_solution(4495602316256039208)
XLA Ops:
  0.0 86.5 %shard_map.17 = f32[1,5,384,384]{3,2,1,0:T(8,128)S(1)} custom-call(bf16[3072,4096]{1,0:T(8,128)(2,1)} %a_hbm.1), custom_call_target="tpu_custom_call" | custom-call | tf_op jit(solution)/shard_map/pallas_call | solution.py:423
  86.5 1.6 %copy.3 = f32[1,5,384,384]{3,2,1,0:T(8,128)} copy(f32[1,5,384,384]{3,2,1,0:T(8,128)S(1)} %shard_map.17) | data formatting | bytes 5898240
